TPU v7x, 32 devices: a 4x4x1 block of a 4x4x8 slice. The times are simulated.
32 devices in a mesh: dp: 1 (over z), dm: 4 (over y), tp: 8 (over x, core).
Axes of the slice: x: 4, y: 4, z: 1, core: 2. Of those that a mesh axis runs over, the one named last changes fastest.
The devices are a block of a 4x4x8 slice.
Arguments:
- hidden: bfloat16 [128, 4096], P('dp', 'dm')
- w_q: bfloat16 [4096, 32, 128], P('dm', 'tp')
- w_k: bfloat16 [4096, 32, 128], P('dm', 'tp')
- w_v: bfloat16 [4096, 32, 128], P('dm', 'tp')
- w_o: bfloat16 [32, 128, 4096], P('tp', None, 'dm')
- w_gate: bfloat16 [4096, 11008], P('dm', 'tp')
- w_up: bfloat16 [4096, 11008], P('dm', 'tp')
- w_down: bfloat16 [11008, 4096], P('tp', 'dm')
- norm_attn: bfloat16 [4096], P('dm')
- norm_mlp: bfloat16 [4096], P('dm')
- k_cache: bfloat16 [128, 256, 32, 128], P(('dp', 'dm'), None, 'tp')
- v_cache: bfloat16 [128, 256, 32, 128], P(('dp', 'dm'), None, 'tp')
- seq_lens: int32 [128], P(('dp', 'dm'))
- rope_cos: float32 [128, 64], P(('dp', 'dm'))
- rope_sin: float32 [128, 64], P(('dp', 'dm'))
Outputs:
- output 1: bfloat16 [128, 4096], P('dp', 'dm')
- output 2: bfloat16 [128, 256, 32, 128], P(('dp', 'dm'), None, 'tp')
- output 3: bfloat16 [128, 256, 32, 128], P(('dp', 'dm'), None, 'tp')
All inputs are finite; a program needn't handle non-finite values.
Results may differ from a plain program's by a relative error of at most 0.0107095.
Values are sent between devices in bfloat16 or wider.
A program may use at most 768 MiB of HBM per device.

v0:
```python
import jax
import jax.numpy as jnp
from jax import lax
from jax.sharding import PartitionSpec as P

EPS = 1e-6


def width_norm(x, gain, width_full):
    x_f32 = x.astype(jnp.float32)
    sq_sum = lax.psum(jnp.sum(x_f32 * x_f32, axis=-1, keepdims=True), 'dm')
    scale = lax.rsqrt(sq_sum / width_full + EPS)
    return (x_f32 * scale * gain.astype(jnp.float32)).astype(jnp.bfloat16)


def apply_rope(x, rope_cos, rope_sin):
    half = x.shape[-1] // 2
    first = x[..., :half]
    second = x[..., half:]
    cosine = rope_cos[:, None, :]
    sine = rope_sin[:, None, :]
    return jnp.concatenate([first * cosine - second * sine, second * cosine + first * sine], axis=-1).astype(jnp.bfloat16)


def attend(q_rot, k_rot, v_new, k_cache, v_cache, seq_lens):
    rows, seq_len, kv_local, head_dim = k_cache.shape
    positions = jnp.arange(seq_len)
    write_mask = (positions[None, :] == seq_lens[:, None])[:, :, None, None]
    k_out = jnp.where(write_mask, k_rot[:, None], k_cache)
    v_out = jnp.where(write_mask, v_new[:, None], v_cache)
    q_grp = q_rot.reshape(rows, kv_local, -1, head_dim)
    scores = jnp.einsum('bkgd,bskd->bkgs', q_grp, k_out, preferred_element_type=jnp.float32) * (head_dim ** -0.5)
    key_mask = (positions[None, :] <= seq_lens[:, None])[:, None, None, :]
    scores = jnp.where(key_mask, scores, -1e30)
    attn_probs = jax.nn.softmax(scores, axis=-1).astype(jnp.bfloat16)
    heads = jnp.einsum('bkgs,bskd->bkgd', attn_probs, v_out, preferred_element_type=jnp.float32)
    return heads.astype(jnp.bfloat16).reshape(rows, -1, head_dim), k_out, v_out


def solution(mesh):
    width_shards = mesh.shape['dm']
    row_spec = P('dp', 'dm')
    cache_spec = P(('dp', 'dm'), None, 'tp', None)
    batch_spec = P(('dp', 'dm'))
    rope_spec = P(('dp', 'dm'), None)
    in_specs = (row_spec, P('dm', 'tp', None), P('dm', 'tp', None), P('dm', 'tp', None), P('tp', None, 'dm'), P('dm', 'tp'), P('dm', 'tp'), P('tp', 'dm'), P('dm'), P('dm'), cache_spec, cache_spec, batch_spec, rope_spec, rope_spec)
    out_specs = (row_spec, cache_spec, cache_spec)

    def local_layer(hidden, w_q, w_k, w_v, w_o, w_gate, w_up, w_down, norm_attn, norm_mlp, k_cache, v_cache, seq_lens, rope_cos, rope_sin):
        width_full = hidden.shape[1] * width_shards
        x_norm = width_norm(hidden, norm_attn, width_full)
        q_part = jnp.einsum('bd,dhk->bhk', x_norm, w_q, preferred_element_type=jnp.float32)
        k_part = jnp.einsum('bd,dhk->bhk', x_norm, w_k, preferred_element_type=jnp.float32)
        v_part = jnp.einsum('bd,dhk->bhk', x_norm, w_v, preferred_element_type=jnp.float32)
        q_rows = lax.psum_scatter(q_part, 'dm', scatter_dimension=0, tiled=True)
        k_rows = lax.psum_scatter(k_part, 'dm', scatter_dimension=0, tiled=True)
        v_rows = lax.psum_scatter(v_part, 'dm', scatter_dimension=0, tiled=True)
        q_rot = apply_rope(q_rows, rope_cos, rope_sin)
        k_rot = apply_rope(k_rows, rope_cos, rope_sin)
        attn_heads, k_out, v_out = attend(q_rot, k_rot, v_rows.astype(jnp.bfloat16), k_cache, v_cache, seq_lens)
        heads_all = lax.all_gather(attn_heads, 'dm', axis=0, tiled=True)
        attn_part = jnp.einsum('bhk,hkd->bd', heads_all, w_o, preferred_element_type=jnp.float32)
        attn_out = lax.psum(attn_part, 'tp').astype(jnp.bfloat16)
        h_mid = hidden + attn_out
        x_mlp = width_norm(h_mid, norm_mlp, width_full)
        gate = lax.psum(jnp.dot(x_mlp, w_gate, preferred_element_type=jnp.float32), 'dm')
        up_proj = lax.psum(jnp.dot(x_mlp, w_up, preferred_element_type=jnp.float32), 'dm')
        gated_act = (jax.nn.silu(gate) * up_proj).astype(jnp.bfloat16)
        mlp_out = lax.psum(jnp.dot(gated_act, w_down, preferred_element_type=jnp.float32), 'tp').astype(jnp.bfloat16)
        return h_mid + mlp_out, k_out, v_out

    return jax.shard_map(local_layer, mesh=mesh, in_specs=in_specs, out_specs=out_specs, check_vma=False)
```

profile of v0, /device:TPU:97, one launch (start us, length us, event | category | flops | bytes accessed | tf_op | source)
XLA Modules:
  0.0 247.6 jit_solution(10336108871147778281)
XLA Ops:
  7.2 0.0 copy-start
  7.2 0.1 reduce-scatter.8.cloned.1.call-start
  7.3 1.2 fusion.17
  8.5 11.2 %psum.42 = f32[128,1]{0,1:T(1,128)S(1)} all-reduce(f32[128,1]{0,1:T(1,128)S(1)} %bitcast.35), channel_id=1, replica_groups=mesh['dp'=1,'dm'=4,'tp'=8] {'dm'}, use_global_device_ids=true, to_apply=%region_1.0 | all-reduce | flops 128 | bytes 1024 | tf_op jit(solution)/shard_map/psum | solution.py:11
  19.7 0.7 convert_element_type.47
  20.4 2.4 fusion.11
  22.8 0.1 reduce-scatter.8.cloned.1.call-update
  22.8 0.1 reduce-scatter.6.cloned.1.call-start
  22.9 2.4 fusion.13
  25.3 0.1 reduce-scatter.6.cloned.1.call-update
  25.4 0.1 reduce-scatter.4.cloned.1.call-start
  25.4 2.4 fusion.15
  27.8 0.1 reduce-scatter.4.cloned.1.call-update
  27.9 0.1 all-reduce.5.cloned.1.call-start
  27.9 0.7 convert_element_type.54
  28.6 0.7 iota_compare_fusion.1
  29.4 11.0 %reduce-scatter.8.cloned.1.call-done = f32[32,4,128]{2,0,1:T(8,128)} async-done(((f32[128,4,128]{2,0,1:T(8,128)}), f32[32,4,128]{2,0,1:T(8,128)}) %reduce-scatter.8.cloned.1.call-update) | async-done | bytes 65552 | tf_op jit(solution)/shard_map/reduce_scatter | solution.py:57
  40.4 0.8 convert_element_type.50
  41.3 20.0 %reduce-scatter.6.cloned.1.call-done = f32[32,4,128]{2,0,1:T(8,128)} async-done(((f32[128,4,128]{2,0,1:T(8,128)}), f32[32,4,128]{2,0,1:T(8,128)}) %reduce-scatter.6.cloned.1.call-update) | async-done | bytes 65552 | tf_op jit(solution)/shard_map/reduce_scatter | solution.py:56
  61.3 20.9 %reduce-scatter.4.cloned.1.call-done = f32[32,4,128]{2,0,1:T(8,128)} async-done(((f32[128,4,128]{2,0,1:T(8,128)}), f32[32,4,128]{2,0,1:T(8,128)}) %reduce-scatter.4.cloned.1.call-update) | async-done | bytes 65552 | tf_op jit(solution)/shard_map/reduce_scatter | solution.py:55
  82.2 1.1 subtract_convert_fusion.1
  83.3 0.1 pad_maximum_fusion
  83.4 0.1 maximum_bitcast_fusion
  83.5 13.7 %broadcast_select_fusion.1 = (bf16[32,256,4,128]{3,2,1,0:T(4,128)(2,1)S(1)}, bf16[32,256,4,128]{3,2,1,0:T(4,128)(2,1)}) fusion(bf16[32,256,4,128]{3,2,1,0:T(4,128)(2,1)} %param.25, pred[32,256]{1,0:T(8,128)(4,1)S(1)} %get-tuple-element.16, bf16[32,4,128]{2,1,0:T(4,128)(2,1)S(1)} %copy.25, bf16[32,256,4,128]{3,2,1,0:T(4,128)(2,1)} %param.26, ...), kind=kLoop, calls=%fused_computation.7 | loop fusion | flops 8388608 | bytes 33628160 | tf_op jit(solution)/shard_map/jit(_where)/select_n | solution.py:29
  97.2 0.0 copy-start.1
  97.2 3.4 %copy-done.1 = bf16[32,256,4,128]{3,2,1,0:T(4,128)(2,1)} copy-done((bf16[32,256,4,128]{3,2,1,0:T(4,128)(2,1)}, bf16[32,256,4,128]{3,2,1,0:T(4,128)(2,1)S(1)}, u32[]{:S(2)}) %copy-start.1) | copy-done | bytes 8388632
  100.6 2.3 fusion.4
  102.9 0.2 fusion.10
  103.1 0.0 copy-start.2
  103.1 4.7 %fusion.2 = bf16[32,4,1,128]{3,2,1,0:T(2,128)(2,1)S(1)} fusion(bf16[32,256,4,128]{3,2,1,0:T(4,128)(2,1)} %get-tuple-element.14, bf16[32,4,256,1]{2,0,1,3:T(8,128)(2,1)S(1)} %fusion.10), kind=kOutput, calls=%fused_computation.2 | convolution fusion | flops 8388608 | bytes 8486912 | tf_op jit(solution)/shard_map/bkgs,bskd->bkgd/dot_general | solution.py:36
  107.8 9.2 %all_gather.3 = bf16[128,4,128]{2,0,1:T(8,128)(2,1)S(1)} all-gather(bf16[32,4,128]{2,0,1:T(8,128)(2,1)S(1)} %bitcast.34), channel_id=1, replica_groups=mesh['dp'=1,'dm'=4,'tp'=8] {'dm'}, dimensions={0}, use_global_device_ids=true | all-gather | bytes 163840 | tf_op jit(solution)/shard_map/all_gather | solution.py:61
  117.0 0.0 copy-done.2
  117.0 0.3 convolution_bitcast_fusion
  117.3 31.9 %all-reduce.6 = bf16[128,1024]{1,0:T(8,128)(2,1)} all-reduce(f32[128,1024]{1,0:T(8,128)S(1)} %convolution_bitcast_fusion), channel_id=1, replica_groups=mesh['dp'=1,'dm'=4,'tp'=8] {'tp'}, use_global_device_ids=true, to_apply=%region_7.8 | all-reduce | flops 131072 | bytes 786432 | tf_op jit(solution)/shard_map/psum | solution.py:63
  149.2 1.2 fusion.20
  150.4 6.5 %psum.44 = f32[128,1]{0,1:T(1,128)S(1)} all-reduce(f32[128,1]{0,1:T(1,128)S(1)} %bitcast.36), channel_id=1, replica_groups=mesh['dp'=1,'dm'=4,'tp'=8] {'dm'}, use_global_device_ids=true, to_apply=%region_9.10 | all-reduce | flops 128 | bytes 1024 | tf_op jit(solution)/shard_map/psum | solution.py:11
  156.9 0.0 copy-done
  156.9 1.9 fusion.30
  158.8 3.6 %fusion.32 = f32[128,1376]{0,1:T(8,128)} fusion(bf16[1024,1376]{0,1:T(8,128)(2,1)} %param.20, bf16[128,1024]{1,0:T(8,128)(2,1)S(1)} %get-tuple-element.6, f32[1024]{0:T(1024)S(1)} %convert_element_type.54, f32[128]{0:T(128)S(1)} %rsqrt_bitcast_fusion), kind=kOutput, calls=%fused_computation.41 | convolution fusion | flops 361234432 | bytes 3789312 | tf_op jit(solution)/shard_map/dot_general | solution.py:66
  162.5 0.1 all-reduce.5.cloned.1.call-update
  162.5 45.4 %all-reduce.5.cloned.1.call-done = (f32[128,1376]{0,1:T(8,128)}, f32[128,1376]{0,1:T(8,128)}) async-done(((f32[128,1376]{0,1:T(8,128)}, f32[128,1376]{0,1:T(8,128)}), (f32[128,1376]{0,1:T(8,128)}, f32[128,1376]{0,1:T(8,128)})) %all-reduce.5.cloned.1.call-update) | async-done | bytes 1409040 | tf_op jit(solution)/shard_map/psum | solution.py:67
  208.0 3.7 %fusion.23 = f32[128,1024]{1,0:T(8,128)} fusion(bf16[1376,1024]{1,0:T(8,128)(2,1)} %param.22, f32[128,1376]{0,1:T(8,128)} %get-tuple-element.3, f32[128,1376]{0,1:T(8,128)} %get-tuple-element.4), kind=kOutput, calls=%fused_computation.31 | convolution fusion | flops 361766912 | bytes 4751360 | tf_op jit(solution)/shard_map/dot_general | solution.py:69
  211.6 28.7 %all-reduce.7 = bf16[128,1024]{1,0:T(8,128)(2,1)S(1)} all-reduce(f32[128,1024]{1,0:T(8,128)} %fusion.23), channel_id=1, replica_groups=mesh['dp'=1,'dm'=4,'tp'=8] {'tp'}, use_global_device_ids=true, to_apply=%region_12.13 | all-reduce | flops 131072 | bytes 786432 | tf_op jit(solution)/shard_map/psum | solution.py:69
  240.3 0.8 add.55
  (5 shorter events, 0.1 us)
Async XLA Ops:
  7.2 149.8 %copy-start = (bf16[1024,1376]{0,1:T(8,128)(2,1)S(1)}, bf16[1024,1376]{0,1:T(8,128)(2,1)}, u32[]{:S(2)}) copy-start(bf16[1024,1376]{0,1:T(8,128)(2,1)} %param.21) | copy-start | bytes 8454148
  7.2 33.2 %reduce-scatter.8.cloned.1.call-start = ((), (), s32[]{:S(2)}) async-start(), calls=%async_computation.5 | async-start | bytes 327680 | tf_op jit(solution)/shard_map/reduce_scatter | solution.py:57
  22.8 38.5 %reduce-scatter.6.cloned.1.call-start = ((), (), s32[]{:S(2)}) async-start(), calls=%async_computation.4 | async-start | bytes 327680 | tf_op jit(solution)/shard_map/reduce_scatter | solution.py:56
  25.4 56.8 %reduce-scatter.4.cloned.1.call-start = ((), (), s32[]{:S(2)}) async-start(), calls=%async_computation.3 | async-start | bytes 327680 | tf_op jit(solution)/shard_map/reduce_scatter | solution.py:55
  27.9 180.1 %all-reduce.5.cloned.1.call-start = ((), (), s32[]{:S(2)}) async-start(), calls=%async_computation.6 | async-start | bytes 2818048 | tf_op jit(solution)/shard_map/psum | solution.py:67
  97.2 3.4 %copy-start.1 = (bf16[32,256,4,128]{3,2,1,0:T(4,128)(2,1)}, bf16[32,256,4,128]{3,2,1,0:T(4,128)(2,1)S(1)}, u32[]{:S(2)}) copy-start(bf16[32,256,4,128]{3,2,1,0:T(4,128)(2,1)S(1)} %get-tuple-element.13) | copy-start | bytes 25165828
  103.1 13.9 %copy-start.2 = (bf16[4,128,1024]{2,1,0:T(8,128)(2,1)S(1)}, bf16[4,128,1024]{2,1,0:T(8,128)(2,1)}, u32[]{:S(2)}) copy-start(bf16[4,128,1024]{2,1,0:T(8,128)(2,1)} %param.19) | copy-start | bytes 3145732
Sparse Core Ops, SparseCore 0:
  23.0 17.3 reduce-scatter.7
  43.2 18.0 reduce-scatter.5
  64.2 18.0 reduce-scatter.3
  162.7 45.2 all-reduce.4
where the time goes:
time: 250 us; the launch traced here: 248 us
  waiting for transfers between devices  97.6 us (39%)
  blocking collectives  87.5 us (35%)
  matrix products  23.5 us (9%)
  other arithmetic  21.4 us (9%)
  between operations  13.9 us (6%)
  local copies, waits for them, and re-layouts  3.46 us (1%)
    psum x1, waiting for transfers between devices, local_layer(): lax.psum(jnp.dot(x_mlp, w_up, preferred_element_type=jnp.float32), 'dm')  45.4 us
    psum x1, blocking collectives, local_layer(): attn_out = lax.psum(attn_part, 'tp').astype(jnp.bfloat16)  31.9 us
    psum x1, blocking collectives, local_layer(): lax.psum(jnp.dot(gated_act, w_down, preferred_element_type=jnp.float32),...  28.7 us
    reduce_scatter x1, waiting for transfers between devices, local_layer(): q_rows = lax.psum_scatter(q_part, 'dm', scatter_dimension=0, tiled=True)  20.9 us
    reduce_scatter x1, waiting for transfers between devices, local_layer(): k_rows = lax.psum_scatter(k_part, 'dm', scatter_dimension=0, tiled=True)  20 us
    psum x2, blocking collectives, width_norm(): sq_sum = lax.psum(jnp.sum(x_f32 * x_f32, axis=-1, keepdims=True), 'dm')  17.8 us
    select_n x1, other arithmetic, attend(): k_out = jnp.where(write_mask, k_rot[:, None], k_cache)  13.7 us
    reduce_scatter x1, waiting for transfers between devices, local_layer(): v_rows = lax.psum_scatter(v_part, 'dm', scatter_dimension=0, tiled=True)  11 us
  transfers between devices with their start and end apart: 4, of which 4 were waited for; matrix products, arithmetic and copies ran while one was open for 3% of the time, Pallas kernels for 0%

commit v1 on v0

v1 whole, which is shorter than its diff:
```python
import functools

import jax
import jax.numpy as jnp
from jax import lax
from jax.experimental import pallas as pl
from jax.experimental.pallas import tpu as pltpu
from jax.sharding import PartitionSpec as P

EPS = 1e-6
MESH = pl.DeviceIdType.MESH
F32 = jnp.float32
BF16 = jnp.bfloat16
NT_DIMS = (((1,), (1,)), ((), ()))
TN_DIMS = (((0,), (0,)), ((), ()))


def remote(src, dst, send_sem, recv_sem, axis, index):
    return pltpu.make_async_remote_copy(
        src_ref=src, dst_ref=dst, send_sem=send_sem, recv_sem=recv_sem,
        device_id={axis: index}, device_id_type=MESH)


def meet(axes):
    barrier = pltpu.get_barrier_semaphore()
    total = 0
    for axis, n in axes:
        me = lax.axis_index(axis)
        for rel in range(1, n):
            pl.semaphore_signal(barrier, inc=1, device_id={axis: lax.rem(me + rel, n)}, device_id_type=MESH)
        total += n - 1
    pl.semaphore_wait(barrier, total)


def column_to_row(col, lanes):
    rows = col.shape[0]
    r = lax.broadcasted_iota(jnp.int32, (rows, lanes), 0)
    c = lax.broadcasted_iota(jnp.int32, (rows, lanes), 1)
    return jnp.sum(jnp.where(r == c, jnp.broadcast_to(col, (rows, lanes)), 0.0), axis=0, keepdims=True)


def row_to_column(row, rows):
    lanes = row.shape[1]
    r = lax.broadcasted_iota(jnp.int32, (rows, lanes), 0)
    c = lax.broadcasted_iota(jnp.int32, (rows, lanes), 1)
    return jnp.sum(jnp.where(r == c, jnp.broadcast_to(row, (rows, lanes)), 0.0), axis=1, keepdims=True)


def qkv_kernel(nd, heads, width_full, hid_ref, gain_ref, wq_ref, wk_ref, wv_ref, cos_ref, sin_ref,
               q_out, k_out, v_out,
               wbuf, w32, wcat, stat, part, sbuf, rbuf,
               wsem, st_ss, st_rs, ss, rs):
    me = lax.axis_index('dm')
    batch, width = hid_ref.shape
    rows = batch // nd
    cols = wcat.shape[2]
    loads = [pltpu.make_async_copy(w, wbuf.at[j], wsem.at[j]) for j, w in enumerate((wq_ref, wk_ref, wv_ref))]
    for load in loads:
        load.start()
    x = hid_ref[...].astype(F32)
    stat[me] = column_to_row(jnp.sum(x * x, axis=1, keepdims=True), batch)
    meet((('dm', nd),))
    st_copies = [remote(stat.at[me], stat.at[me], st_ss.at[rel], st_rs.at[rel], 'dm', lax.rem(me + rel, nd)) for rel in range(1, nd)]
    for copy in st_copies:
        copy.start()
    step = width // 8
    for j in range(3):
        loads[j].wait()

        @pl.loop(0, 8)
        def _(c, j=j):
            src = pl.multiple_of(c * step * heads, step * heads)
            w32[...] = wbuf[j, pl.ds(src, step * heads), :].astype(F32)
            dst = pl.multiple_of(c * step, step)
            for h in range(heads):
                wcat[j, pl.ds(dst, step), h * 128:(h + 1) * 128] = w32[pl.ds(h, step, stride=heads), :].astype(BF16)
    for copy in st_copies:
        copy.wait()
    total = stat[0]
    for i in range(1, nd):
        total = total + stat[i]
    scale = lax.rsqrt(row_to_column(total, batch) / width_full + EPS)
    gain = gain_ref[...].astype(F32)
    x_norm = (x * scale * gain).astype(BF16)
    copies = []
    for j in range(3):
        out = jnp.dot(x_norm, wcat[j], preferred_element_type=F32)
        for i in range(nd):
            part[j, i] = out[i * rows:(i + 1) * rows]
            sbuf[j, i] = out[i * rows:(i + 1) * rows].astype(BF16)
        for rel in (2, 1, 3) if nd == 4 else range(1, nd):
            to = lax.rem(me + rel, nd)
            copy = remote(sbuf.at[j, to], rbuf.at[j, me], ss.at[j, rel], rs.at[j, rel], 'dm', to)
            copy.start()
            copies.append(copy)
    cos = cos_ref[...]
    sin = sin_ref[...]
    cos = jnp.concatenate([cos, cos], axis=1)
    sin = jnp.concatenate([-sin, sin], axis=1)
    for j in range(3):
        for copy in copies[j * (nd - 1):(j + 1) * (nd - 1)]:
            copy.wait_recv()
        total = part[j, me]
        for rel in range(1, nd):
            total = total + rbuf[j, lax.rem(me + nd - rel, nd)].astype(F32)
        for h in range(heads):
            v = total[:, h * 128:(h + 1) * 128]
            if j < 2:
                v = v * cos + pltpu.roll(v, 64, 1) * sin
            v = v.astype(BF16).astype(F32)
            if j == 0:
                q_out[:, h] = v.reshape(rows // 8, 8, 128)
            elif j == 1:
                k_out[h] = v
            else:
                v_out[h] = v
    for copy in copies:
        copy.wait_send()


def attend_kernel(len_ref, q_ref, knew_ref, vnew_ref, k_hbm, v_hbm, o_ref, k_hbm_out, v_hbm_out,
                  k_buf, v_buf, new, new16, o32, in_sem, out_sem):
    groups, heads, gb, dim = q_ref.shape
    rows, span, _ = k_hbm.shape

    def copy_in(g, j):
        at = pl.ds(g * gb, gb)
        return pltpu.make_async_copy((k_hbm, v_hbm)[j].at[at], (k_buf, v_buf)[j].at[at], in_sem.at[j, g])

    def copy_out(g, j):
        at = pl.ds(g * gb, gb)
        return pltpu.make_async_copy((k_buf, v_buf)[j].at[at], (k_hbm_out, v_hbm_out)[j].at[at], out_sem.at[j, g])

    for g in range(groups):
        for j in range(2):
            copy_in(g, j).start()
    lane = lax.broadcasted_iota(jnp.int32, (heads * gb, span), 1)
    row = lax.broadcasted_iota(jnp.int32, (heads * gb, span), 0)
    head_ok = lane % heads == row // gb
    slot = lane // heads
    row1 = lax.broadcasted_iota(jnp.int32, (heads * gb, 128), 0)
    r16 = lax.broadcasted_iota(jnp.int32, (16, 128), 0) // heads
    per = 16 // heads
    for j, src in enumerate((knew_ref, vnew_ref)):
        for h in range(heads):
            for s in range(per):
                new[pl.ds(s * heads + h, rows, stride=16), :] = src[h]
        new16[j] = new[...].astype(BF16)

    @pl.loop(0, groups)
    def _(g):
        for j in range(2):
            copy_in(g, j).wait()
        lens = jnp.zeros((heads * gb, 128), jnp.int32)
        for b8 in range(gb):
            b = g * gb + b8
            n = len_ref[b]
            lens = jnp.where(row1 % gb == b8, n, lens)
            at = pl.ds(pl.multiple_of((n // per) * 16, 16), 16)
            hit = r16 == n % per
            src = pl.ds(pl.multiple_of(b * 16, 16), 16)
            for j, cache in enumerate((k_buf, v_buf)):
                old = cache[b, at, :].astype(F32)
                cache[b, at, :] = jnp.where(hit, new16[j, src, :].astype(F32), old).astype(BF16)
        q = jnp.concatenate([q_ref[g, h] for h in range(heads)], axis=0)
        q_exp = jnp.concatenate([jnp.where(row1 % gb == b8, q, 0.0).astype(BF16) for b8 in range(gb)], axis=1)
        parts = []
        for nb in range(span // 256):
            keys = jnp.concatenate([k_buf[g * gb + b8, nb * 256:(nb + 1) * 256, :] for b8 in range(gb)], axis=1)
            parts.append(lax.dot_general(q_exp, keys, NT_DIMS, preferred_element_type=F32))
        s = jnp.concatenate(parts, axis=1) * (dim ** -0.5)
        ok = head_ok & (slot <= jnp.concatenate([lens] * (span // 128), axis=1))
        s = jnp.where(ok, s, -1e30)
        top = jnp.max(s, axis=1, keepdims=True)
        e = jnp.where(ok, jnp.exp(s - top), 0.0)
        p = (e / jnp.sum(e, axis=1, keepdims=True))
        acc = jnp.zeros((heads * gb, 2 * dim), F32)
        half = gb // 2
        for pair in range(half):
            p_pair = jnp.where(row % half == pair, p, 0.0).astype(BF16)
            vals = jnp.concatenate([v_buf[g * gb + pair], v_buf[g * gb + pair + half]], axis=1)
            acc = acc + jnp.dot(p_pair, vals, preferred_element_type=F32)
        o = jnp.where(row1 % gb < half, acc[:, :dim], acc[:, dim:])
        for h in range(heads):
            o32[pl.ds(pl.multiple_of(g * gb, gb), gb), h * dim:(h + 1) * dim] = o[h * gb:(h + 1) * gb]
        for j in range(2):
            copy_out(g, j).start()

    o_ref[...] = o32[...].astype(BF16)
    for g in range(groups):
        for j in range(2):
            copy_out(g, j).wait()


def mlp_kernel(nd, nt, fc, width_full, o_ref, hid_ref, gain_ref, wo_hbm, wg_hbm, wu_hbm, wd_hbm, out_ref,
               wo, wg, wu, wd, o_all, acc32, rs1_s, rs1_r, mid, st_dm, st_tp, x2, gu_s, gu_r, gu_own, m_all,
               rs2_s, rs2_r, fin,
               wsem, o_ss, o_rs, a_ss, a_rs, b_ss, b_rs, sd_ss, sd_rs, st_ss, st_rs, g_ss, g_rs, m_ss, m_rs,
               c_ss, c_rs, d_ss, d_rs):
    dm = lax.axis_index('dm')
    tp = lax.axis_index('tp')
    rows_d = o_ref.shape[0]
    rows_t = mid.shape[1]
    per = rows_d // rows_t
    width = hid_ref.shape[1]
    ff = wg_hbm.shape[0]
    sends = []
    wloads = [pltpu.make_async_copy(wo_hbm, wo, wsem.at[0]),
              pltpu.make_async_copy(wg_hbm, wg.at[pl.ds(0, ff)], wsem.at[1]),
              pltpu.make_async_copy(wu_hbm, wu.at[pl.ds(0, ff)], wsem.at[2]),
              pltpu.make_async_copy(wd_hbm, wd.at[pl.ds(0, ff)], wsem.at[3])]
    for load in wloads:
        load.start()
    meet((('dm', nd), ('tp', nt)))
    o_copies = {}
    for rel in (2, 1, 3) if nd == 4 else range(1, nd):
        to = lax.rem(dm + rel, nd)
        o_copies[rel] = remote(o_ref, o_all.at[dm], o_ss.at[rel], o_rs.at[rel], 'dm', to)
        o_copies[rel].start()
        sends.append(o_copies[rel])
    if wg.shape[0] > ff:
        for w in (wg, wu, wd):
            w[ff:, :] = jnp.zeros((w.shape[0] - ff, width), BF16)
    wloads[0].wait()
    for rel in range(nd):
        j = lax.rem(dm + nd - rel, nd)
        if rel:
            o_copies[rel].wait_recv()
            o = o_all[j]
        else:
            o = o_ref[...]
        part = jnp.dot(o, wo[...], preferred_element_type=F32)
        for c in range(per):
            t = j * per + c
            acc32[t] = part[c * rows_t:(c + 1) * rows_t]
            rs1_s[t] = part[c * rows_t:(c + 1) * rows_t].astype(BF16)
            far = lax.rem(t + nt - tp, nt)

            @pl.when(far != 0)
            def _(t=t, far=far):
                remote(rs1_s.at[t], rs1_r.at[tp], a_ss.at[far], a_rs.at[far], 'tp', t).start()

    def reduced(acc, recv, s_sems, r_sems, sent):
        total = acc[tp]
        for rel in range(1, nt):
            frm = lax.rem(tp + nt - rel, nt)
            copy = remote(sent.at[frm], recv.at[frm], s_sems.at[rel], r_sems.at[rel], 'tp', frm)
            copy.wait_recv()
            total = total + recv[frm].astype(F32)
            sends.append(copy)
        return total.astype(BF16)

    def gather(buf, s_sems, r_sems):
        out = {}
        for rel in range(1, nt):
            out[rel] = remote(buf.at[tp], buf.at[tp], s_sems.at[rel], r_sems.at[rel], 'tp', lax.rem(tp + rel, nt))
            out[rel].start()
            sends.append(out[rel])
        return out

    attn = reduced(acc32, rs1_r, a_ss, a_rs, rs1_s)
    hid = hid_ref[pl.ds(pl.multiple_of(tp * rows_t, rows_t), rows_t), :]
    mine = (hid.astype(F32) + attn.astype(F32)).astype(BF16)
    mid[tp] = mine
    mid_copies = gather(mid, b_ss, b_rs)
    y = mine.astype(F32)
    st_dm[dm] = column_to_row(jnp.sum(y * y, axis=1, keepdims=True), 128)
    sd_copies = []
    for rel in range(1, nd):
        copy = remote(st_dm.at[dm], st_dm.at[dm], sd_ss.at[rel], sd_rs.at[rel], 'dm', lax.rem(dm + rel, nd))
        copy.start()
        sd_copies.append(copy)
    sends.extend(sd_copies)
    for copy in sd_copies:
        copy.wait_recv()
    total = st_dm[0]
    for i in range(1, nd):
        total = total + st_dm[i]
    st_tp[tp] = total
    st_copies = gather(st_tp, st_ss, st_rs)
    gain = gain_ref[...].astype(F32)
    for rel in range(nt):
        t = lax.rem(tp + nt - rel, nt)
        if rel:
            st_copies[rel].wait_recv()
            mid_copies[rel].wait_recv()
        scale = lax.rsqrt(row_to_column(st_tp[t], rows_t) / width_full + EPS)
        x2[pl.ds(pl.multiple_of(t * rows_t, rows_t), rows_t), :] = (mid[t].astype(F32) * scale * gain).astype(BF16)
    wloads[1].wait()
    wloads[2].wait()
    g_copies = {}
    for rel in (2, 1, 3, 0) if nd == 4 else [*range(1, nd), 0]:
        to = lax.rem(dm + rel, nd)
        at = pl.ds(pl.multiple_of(to * fc, 16), fc)
        for i, w in enumerate((wg, wu)):
            part = lax.dot_general(w[at, :], x2[...], NT_DIMS, preferred_element_type=F32)
            if rel:
                gu_s[to, i] = part.astype(BF16)
            else:
                gu_own[i] = part
        if rel:
            g_copies[rel] = remote(gu_s.at[to], gu_r.at[dm], g_ss.at[rel], g_rs.at[rel], 'dm', to)
            g_copies[rel].start()
            sends.append(g_copies[rel])
    gate = gu_own[0]
    up = gu_own[1]
    for rel in (1, 3, 2) if nd == 4 else range(1, nd):
        frm = lax.rem(dm + nd - rel, nd)
        g_copies[rel].wait_recv()
        gate = gate + gu_r[frm, 0].astype(F32)
        up = up + gu_r[frm, 1].astype(F32)
    m_all[dm] = (gate / (1.0 + jnp.exp(-gate)) * up).astype(BF16)
    m_copies = {}
    for rel in (2, 1, 3) if nd == 4 else range(1, nd):
        m_copies[rel] = remote(m_all.at[dm], m_all.at[dm], m_ss.at[rel], m_rs.at[rel], 'dm', lax.rem(dm + rel, nd))
        m_copies[rel].start()
        sends.append(m_copies[rel])
    wloads[3].wait()
    for k, rel in enumerate((0, 1, 3, 2) if nd == 4 else range(nd)):
        j = lax.rem(dm + nd - rel, nd)
        if rel:
            m_copies[rel].wait_recv()
        part = lax.dot_general(m_all[j], wd[pl.ds(pl.multiple_of(j * fc, 16), fc), :], TN_DIMS, preferred_element_type=F32)
        for t in range(nt):
            piece = part[t * rows_t:(t + 1) * rows_t]
            acc32[t] = piece if k == 0 else acc32[t] + piece
    for t in range(nt):
        rs2_s[t] = acc32[t].astype(BF16)
    for rel in range(1, nt):
        to = lax.rem(tp + rel, nt)
        remote(rs2_s.at[to], rs2_r.at[tp], c_ss.at[rel], c_rs.at[rel], 'tp', to).start()
    mlp = reduced(acc32, rs2_r, c_ss, c_rs, rs2_s)
    fin[tp] = (mid[tp].astype(F32) + mlp.astype(F32)).astype(BF16)
    f_copies = gather(fin, d_ss, d_rs)
    for rel in range(nt):
        t = lax.rem(tp + nt - rel, nt)
        if rel:
            f_copies[rel].wait_recv()
        out_ref[pl.ds(pl.multiple_of(t * rows_t, rows_t), rows_t), :] = fin[t]
    for copy in sends:
        copy.wait_send()


VMEM = pl.BlockSpec(memory_space=pltpu.VMEM)
SMEM = pl.BlockSpec(memory_space=pltpu.SMEM)
HBM = pl.BlockSpec(memory_space=pltpu.HBM)
MIB = 1 << 20


def solution(mesh):
    nd = mesh.shape['dm']
    nt = mesh.shape['tp']
    row_spec = P('dp', 'dm')
    cache_spec = P(('dp', 'dm'), None, 'tp', None)
    batch_spec = P(('dp', 'dm'))
    rope_spec = P(('dp', 'dm'), None)
    in_specs = (row_spec, P('dm', 'tp', None), P('dm', 'tp', None), P('dm', 'tp', None), P('tp', None, 'dm'), P('dm', 'tp'), P('dm', 'tp'), P('tp', 'dm'), P('dm'), P('dm'), cache_spec, cache_spec, batch_spec, rope_spec, rope_spec)
    out_specs = (row_spec, cache_spec, cache_spec)
    dma = pltpu.SemaphoreType.DMA

    def local_layer(hidden, w_q, w_k, w_v, w_o, w_gate, w_up, w_down, norm_attn, norm_mlp, k_cache, v_cache, seq_lens, rope_cos, rope_sin):
        batch, width = hidden.shape
        width_full = width * nd
        _, heads, dim = w_q.shape
        rows, seq = k_cache.shape[:2]
        cols = heads * dim
        ff = w_gate.shape[1]
        def hbm(x):
            return pltpu.with_memory_space_constraint(x, pltpu.HBM)

        q, k, v = pl.pallas_call(
            functools.partial(qkv_kernel, nd, heads, width_full),
            out_shape=(jax.ShapeDtypeStruct((rows // 8, heads, 8, dim), F32),
                       jax.ShapeDtypeStruct((heads, rows, dim), F32),
                       jax.ShapeDtypeStruct((heads, rows, dim), F32)),
            in_specs=[VMEM, VMEM, HBM, HBM, HBM, VMEM, VMEM],
            out_specs=(VMEM, VMEM, VMEM),
            scratch_shapes=[
                pltpu.VMEM((3, width * heads, dim), BF16),
                pltpu.VMEM((width // 8 * heads, dim), F32),
                pltpu.VMEM((3, width, cols), BF16),
                pltpu.VMEM((nd, 1, batch), F32),
                pltpu.VMEM((3, nd, rows, cols), F32),
                pltpu.VMEM((3, nd, rows, cols), BF16),
                pltpu.VMEM((3, nd, rows, cols), BF16),
                dma((3,)), dma((nd,)), dma((nd,)), dma((3, nd)), dma((3, nd)),
            ],
            compiler_params=pltpu.CompilerParams(collective_id=0, has_side_effects=True, vmem_limit_bytes=16 * MIB),
            name='qkv',
        )(hidden, norm_attn.reshape(1, width), hbm(w_q.reshape(width * heads, dim)), hbm(w_k.reshape(width * heads, dim)),
          hbm(w_v.reshape(width * heads, dim)), rope_cos, rope_sin)

        flat = (rows, seq * heads, dim)
        o, k_new, v_new = pl.pallas_call(
            attend_kernel,
            out_shape=(jax.ShapeDtypeStruct((rows, cols), BF16),
                       jax.ShapeDtypeStruct(flat, BF16),
                       jax.ShapeDtypeStruct(flat, BF16)),
            in_specs=[SMEM, VMEM, VMEM, VMEM, HBM, HBM],
            out_specs=(VMEM, HBM, HBM),
            scratch_shapes=[
                pltpu.VMEM(flat, BF16),
                pltpu.VMEM(flat, BF16),
                pltpu.VMEM((rows * 16, dim), F32),
                pltpu.VMEM((2, rows * 16, dim), BF16),
                pltpu.VMEM((rows, cols), F32),
                dma((2, rows // 8)), dma((2, rows // 8)),
            ],
            compiler_params=pltpu.CompilerParams(vmem_limit_bytes=40 * MIB),
            name='attend',
        )(seq_lens, q, k, v, hbm(k_cache.reshape(flat)), hbm(v_cache.reshape(flat)))

        fc = -(-ff // (nd * 16)) * 16
        rows_t = batch // nt
        slab = (nt, rows_t, width)
        out = pl.pallas_call(
            functools.partial(mlp_kernel, nd, nt, fc, width_full),
            out_shape=jax.ShapeDtypeStruct((batch, width), BF16),
            in_specs=[VMEM, VMEM, VMEM, HBM, HBM, HBM, HBM],
            out_specs=VMEM,
            scratch_shapes=[
                pltpu.VMEM((cols, width), BF16),
                pltpu.VMEM((nd * fc, width), BF16),
                pltpu.VMEM((nd * fc, width), BF16),
                pltpu.VMEM((nd * fc, width), BF16),
                pltpu.VMEM((nd, rows, cols), BF16),
                pltpu.VMEM(slab, F32),
                pltpu.VMEM(slab, BF16),
                pltpu.VMEM(slab, BF16),
                pltpu.VMEM(slab, BF16),
                pltpu.VMEM((nd, 1, 128), F32),
                pltpu.VMEM((nt, 1, 128), F32),
                pltpu.VMEM((batch, width), BF16),
                pltpu.VMEM((nd, 2, fc, batch), BF16),
                pltpu.VMEM((nd, 2, fc, batch), BF16),
                pltpu.VMEM((2, fc, batch), F32),
                pltpu.VMEM((nd, fc, batch), BF16),
                pltpu.VMEM(slab, BF16),
                pltpu.VMEM(slab, BF16),
                pltpu.VMEM(slab, BF16),
                dma((4,)), dma((nd,)), dma((nd,)), dma((nt,)), dma((nt,)), dma((nt,)), dma((nt,)),
                dma((nd,)), dma((nd,)), dma((nt,)), dma((nt,)), dma((nd,)), dma((nd,)), dma((nd,)), dma((nd,)),
                dma((nt,)), dma((nt,)), dma((nt,)), dma((nt,)),
            ],
            compiler_params=pltpu.CompilerParams(collective_id=1, has_side_effects=True, vmem_limit_bytes=24 * MIB),
            name='mlp',
        )(o, hidden, norm_mlp.reshape(1, width), hbm(w_o.reshape(cols, width)), hbm(w_gate.T), hbm(w_up.T), hbm(w_down))
        return out, k_new.reshape(k_cache.shape), v_new.reshape(v_cache.shape)

    return jax.shard_map(local_layer, mesh=mesh, in_specs=in_specs, out_specs=out_specs, check_vma=False)
```

time: 250 us -> 84.1 us (0.34)
  waiting for transfers between devices: 97.6 us -> 0 us
  blocking collectives: 87.5 us -> 0 us
  Pallas kernels: 0 us -> 78 us
  matrix products: 23.5 us -> 0 us
  other arithmetic: 21.4 us -> 0 us
  between operations: 13.9 us -> 0.67 us
    psum x4 -> x0, blocking collectives: 78.3 us -> none  [the longest x1 31.9 us: local_layer(): attn_out = lax.psum(attn_part, 'tp').astype(jnp.bfloat16)]
    pallas_call x0 -> x3, Pallas kernels: none -> 78 us  [the longest x1 50.7 us: local_layer(): pl.pallas_call(functools.partial(mlp_kernel, nd, nt, fc, width_full), out...]
    reduce_scatter x3 -> x0, waiting for transfers between devices: 52 us -> none  [the longest x1 20.9 us: local_layer(): q_rows = lax.psum_scatter(q_part, 'dm', scatter_dimension=0, tiled=True)]
    psum x1 -> x0, waiting for transfers between devices: 45.4 us -> none  [local_layer(): lax.psum(jnp.dot(x_mlp, w_up, preferred_element_type=jnp.float32), 'dm')]
    dot_general x9 -> x0, matrix products: 23.5 us -> none  [the longest x1 4.66 us: attend(): jnp.einsum('bkgs,bskd->bkgd', attn_probs, v_out, preferred_element_type=j...]
    select_n x1 -> x0, other arithmetic: 13.7 us -> none  [attend(): k_out = jnp.where(write_mask, k_rot[:, None], k_cache)]
    all_gather x1 -> x0, blocking collectives: 9.16 us -> none  [local_layer(): heads_all = lax.all_gather(attn_heads, 'dm', axis=0, tiled=True)]
  transfers between devices with their start and end apart: 4 -> 0, of which waited for: 4 -> 0; matrix products, arithmetic and copies ran while one was open for 3% -> 0% of each run, Pallas kernels for 0% -> 0%
where the time goes in v1:
time: 84.1 us; the launch traced here: 83.8 us
  Pallas kernels  78 us (93%)
  local copies, waits for them, and re-layouts  5.11 us (6%)
    pallas_call x1, Pallas kernels, local_layer(): pl.pallas_call(functools.partial(mlp_kernel, nd, nt, fc, width_full), out...  50.7 us
    pallas_call x1, Pallas kernels, local_layer(): pl.pallas_call(functools.partial(qkv_kernel, nd, heads, width_full), out_...  13.9 us
    pallas_call x1, Pallas kernels, local_layer(): pl.pallas_call(attend_kernel, out_shape=(jax.ShapeDtypeStruct((rows, cols...  13.4 us
    unnamed x11, local copies, waits for them, and re-layouts  3.74 us

profile of v1, /device:TPU:97, one launch (start us, length us, event | category | flops | bytes accessed | tf_op | source)
XLA Modules:
  0.0 83.8 jit_solution(3746829176232566403)
XLA Ops:
  0.6 0.7 reshape.36.gain_ref
  1.3 0.7 reshape.42.gain_ref
  2.0 0.0 copy-start
  2.0 0.9 %copy-done = bf16[128,1024]{1,0:T(8,128)(2,1)S(1)} copy-done((bf16[128,1024]{1,0:T(8,128)(2,1)S(1)}, bf16[128,1024]{1,0:T(8,128)(2,1)}, u32[]{:S(2)}) %copy-start) | copy-done | bytes 262168
  3.0 0.0 copy-start.2
  3.0 0.7 copy-done.2
  3.7 0.0 copy-start.3
  3.7 0.7 copy-done.3
  4.4 13.9 %qkv.1 = (f32[4,4,8,128]{3,2,1,0:T(8,128)S(1)}, f32[4,32,128]{2,1,0:T(8,128)S(1)}, f32[4,32,128]{2,1,0:T(8,128)S(1)}) custom-call(bf16[128,1024]{1,0:T(8,128)(2,1)S(1)} %copy-done, bf16[1,1024]{1,0:T(2,128)(2,1)S(1)} %reshape.36.gain_ref, bf16[4096,128]{1,0:T(8,128)(2,1)} %bitcast.15, bf16[4096,128]{1,0:T(8,128)(2,1)} %bitcast.16, ...), custom_call_target="tpu_custom_call" | custom-call | tf_op jit(solution)/shard_map/qkv/pallas_call | solution.py:371
  18.3 0.0 copy-start.4
  18.3 0.6 copy-done.4
  19.0 0.0 copy-start.1
  19.0 13.4 %attend.1 = (bf16[32,512]{1,0:T(8,128)(2,1)S(1)}, bf16[32,1024,128]{2,1,0:T(8,128)(2,1)}, bf16[32,1024,128]{2,1,0:T(8,128)(2,1)}) custom-call(s32[32]{0:T(128)S(1)} %copy-done.4, f32[4,4,8,128]{3,2,1,0:T(8,128)S(1)} %get-tuple-element.9.q_ref, f32[4,32,128]{2,1,0:T(8,128)S(1)} %get-tuple-element.10.knew_ref, f32[4,32,128]{2,1,0:T(8,128)S(1)} %get-tuple-element.11.vnew_ref, ...), custom_call_target="tpu_custom_call" | custom-call | tf_op jit(solution)/shard_map/attend/pallas_call | solution.py:394
  32.4 0.0 copy-done.1
  32.4 50.7 %mlp.1 = bf16[128,1024]{1,0:T(8,128)(2,1)S(1)} custom-call(bf16[32,512]{1,0:T(8,128)(2,1)S(1)} %get-tuple-element.12.o_ref, bf16[128,1024]{1,0:T(8,128)(2,1)S(1)} %copy-done.1, bf16[1,1024]{1,0:T(2,128)(2,1)S(1)} %reshape.42.gain_ref, bf16[512,1024]{1,0:T(8,128)(2,1)} %bitcast.14, bf16[1376,1024]{1,0:T(8,128)(2,1)} %bitcast.12, bf16[1376,1024]{1,0:T(8,128)(2,1)} %bitcast.13, ...), custom_call_target="tpu_custom_call" | custom-call | tf_op jit(solution)/shard_map/mlp/pallas_call | solution.py:416
  83.0 0.7 copy.19
Async XLA Ops:
  2.0 0.9 %copy-start = (bf16[128,1024]{1,0:T(8,128)(2,1)S(1)}, bf16[128,1024]{1,0:T(8,128)(2,1)}, u32[]{:S(2)}) copy-start(bf16[128,1024]{1,0:T(8,128)(2,1)} %hid_ref.3) | copy-start | bytes 786436
  3.0 0.7 copy-start.2
  3.7 0.7 copy-start.3
  18.3 0.7 copy-start.4
  19.0 13.4 %copy-start.1 = (bf16[128,1024]{1,0:T(8,128)(2,1)S(1)}, bf16[128,1024]{1,0:T(8,128)(2,1)}, u32[]{:S(2)}) copy-start(bf16[128,1024]{1,0:T(8,128)(2,1)} %hid_ref.3) | copy-start | bytes 786436

commit v2 on v1

--- a/solution.py
+++ b/solution.py
@@ -46,17 +46,22 @@
     return jnp.sum(jnp.where(r == c, jnp.broadcast_to(row, (rows, lanes)), 0.0), axis=1, keepdims=True)
 
 
-def qkv_kernel(nd, heads, width_full, hid_ref, gain_ref, wq_ref, wk_ref, wv_ref, cos_ref, sin_ref,
+def qkv_kernel(nd, heads, width_full, hid_hbm, gain_hbm, wq_ref, wk_ref, wv_ref, cos_hbm, sin_hbm,
                q_out, k_out, v_out,
-               wbuf, w32, wcat, stat, part, sbuf, rbuf,
-               wsem, st_ss, st_rs, ss, rs):
+               hid_ref, gain_ref, cos_ref, sin_ref, wbuf, w32, wcat, stat, part, sbuf, rbuf,
+               isem, wsem, st_ss, st_rs, ss, rs):
     me = lax.axis_index('dm')
     batch, width = hid_ref.shape
     rows = batch // nd
-    cols = wcat.shape[2]
+    small = [pltpu.make_async_copy(src, dst, isem.at[i]) for i, (src, dst) in enumerate(
+        ((hid_hbm, hid_ref), (gain_hbm, gain_ref), (cos_hbm, cos_ref), (sin_hbm, sin_ref)))]
+    for load in small:
+        load.start()
     loads = [pltpu.make_async_copy(w, wbuf.at[j], wsem.at[j]) for j, w in enumerate((wq_ref, wk_ref, wv_ref))]
     for load in loads:
         load.start()
+    for load in small:
+        load.wait()
     x = hid_ref[...].astype(F32)
     stat[me] = column_to_row(jnp.sum(x * x, axis=1, keepdims=True), batch)
     meet((('dm', nd),))
@@ -80,7 +85,7 @@
     for i in range(1, nd):
         total = total + stat[i]
     scale = lax.rsqrt(row_to_column(total, batch) / width_full + EPS)
-    gain = gain_ref[...].astype(F32)
+    gain = gain_ref[...].astype(F32).reshape(1, width)
     x_norm = (x * scale * gain).astype(BF16)
     copies = []
     for j in range(3):
@@ -118,82 +123,90 @@
         copy.wait_send()
 
 
-def attend_kernel(len_ref, q_ref, knew_ref, vnew_ref, k_hbm, v_hbm, o_ref, k_hbm_out, v_hbm_out,
-                  k_buf, v_buf, new, new16, o32, in_sem, out_sem):
+def attend_kernel(len_ref, q_ref, knew_ref, vnew_ref, k_buf, v_buf, o_ref, k_out, v_out, new, patch, o32, out_sem, patch_sem):
     groups, heads, gb, dim = q_ref.shape
-    rows, span, _ = k_hbm.shape
-
-    def copy_in(g, j):
+    rows, span, _ = k_buf.shape
+    per = 16 // heads
+    caches = ((k_buf, k_out), (v_buf, v_out))
+
+    def bulk(g, j):
         at = pl.ds(g * gb, gb)
-        return pltpu.make_async_copy((k_hbm, v_hbm)[j].at[at], (k_buf, v_buf)[j].at[at], in_sem.at[j, g])
-
-    def copy_out(g, j):
-        at = pl.ds(g * gb, gb)
-        return pltpu.make_async_copy((k_buf, v_buf)[j].at[at], (k_hbm_out, v_hbm_out)[j].at[at], out_sem.at[j, g])
+        return pltpu.make_async_copy(caches[j][0].at[at], caches[j][1].at[at], out_sem.at[j, g])
+
+    def patch_copy(b, j):
+        at = pl.ds(pl.multiple_of((len_ref[b] // per) * 16, 16), 16)
+        return pltpu.make_async_copy(patch.at[j, b], caches[j][1].at[b, at], patch_sem.at[j, b])
 
     for g in range(groups):
         for j in range(2):
-            copy_in(g, j).start()
+            bulk(g, j).start()
     lane = lax.broadcasted_iota(jnp.int32, (heads * gb, span), 1)
     row = lax.broadcasted_iota(jnp.int32, (heads * gb, span), 0)
     head_ok = lane % heads == row // gb
     slot = lane // heads
-    row1 = lax.broadcasted_iota(jnp.int32, (heads * gb, 128), 0)
-    r16 = lax.broadcasted_iota(jnp.int32, (16, 128), 0) // heads
-    per = 16 // heads
+    row1 = lax.broadcasted_iota(jnp.int32, (heads * gb, dim), 0)
+    r16 = lax.broadcasted_iota(jnp.int32, (16, dim), 0) // heads
     for j, src in enumerate((knew_ref, vnew_ref)):
         for h in range(heads):
             for s in range(per):
-                new[pl.ds(s * heads + h, rows, stride=16), :] = src[h]
-        new16[j] = new[...].astype(BF16)
+                new[j, pl.ds(s * heads + h, rows, stride=16), :] = src[h]
 
     @pl.loop(0, groups)
     def _(g):
-        for j in range(2):
-            copy_in(g, j).wait()
-        lens = jnp.zeros((heads * gb, 128), jnp.int32)
+        lens = jnp.zeros((heads * gb, dim), jnp.int32)
         for b8 in range(gb):
             b = g * gb + b8
             n = len_ref[b]
             lens = jnp.where(row1 % gb == b8, n, lens)
             at = pl.ds(pl.multiple_of((n // per) * 16, 16), 16)
-            hit = r16 == n % per
             src = pl.ds(pl.multiple_of(b * 16, 16), 16)
-            for j, cache in enumerate((k_buf, v_buf)):
-                old = cache[b, at, :].astype(F32)
-                cache[b, at, :] = jnp.where(hit, new16[j, src, :].astype(F32), old).astype(BF16)
+            for j in range(2):
+                old = caches[j][0][b, at, :].astype(F32)
+                patch[j, b] = jnp.where(r16 == n % per, new[j, src, :], old).astype(BF16)
+        mine = pl.ds(pl.multiple_of(g * gb, gb), gb)
         q = jnp.concatenate([q_ref[g, h] for h in range(heads)], axis=0)
+        k_new = jnp.concatenate([knew_ref[h, mine, :] for h in range(heads)], axis=0)
+        v_new = jnp.concatenate([vnew_ref[h, mine, :] for h in range(heads)], axis=0)
         q_exp = jnp.concatenate([jnp.where(row1 % gb == b8, q, 0.0).astype(BF16) for b8 in range(gb)], axis=1)
         parts = []
         for nb in range(span // 256):
             keys = jnp.concatenate([k_buf[g * gb + b8, nb * 256:(nb + 1) * 256, :] for b8 in range(gb)], axis=1)
             parts.append(lax.dot_general(q_exp, keys, NT_DIMS, preferred_element_type=F32))
         s = jnp.concatenate(parts, axis=1) * (dim ** -0.5)
-        ok = head_ok & (slot <= jnp.concatenate([lens] * (span // 128), axis=1))
+        s_new = jnp.sum(q * k_new, axis=1, keepdims=True) * (dim ** -0.5)
+        ok = head_ok & (slot < jnp.concatenate([lens] * (span // dim), axis=1))
         s = jnp.where(ok, s, -1e30)
-        top = jnp.max(s, axis=1, keepdims=True)
+        top = jnp.maximum(jnp.max(s, axis=1, keepdims=True), s_new)
         e = jnp.where(ok, jnp.exp(s - top), 0.0)
-        p = (e / jnp.sum(e, axis=1, keepdims=True))
+        e_new = jnp.exp(s_new - top)
+        total = jnp.sum(e, axis=1, keepdims=True) + e_new
+        p = e / total
+        p_new = (e_new / total).astype(BF16).astype(F32)
         acc = jnp.zeros((heads * gb, 2 * dim), F32)
         half = gb // 2
         for pair in range(half):
             p_pair = jnp.where(row % half == pair, p, 0.0).astype(BF16)
             vals = jnp.concatenate([v_buf[g * gb + pair], v_buf[g * gb + pair + half]], axis=1)
             acc = acc + jnp.dot(p_pair, vals, preferred_element_type=F32)
-        o = jnp.where(row1 % gb < half, acc[:, :dim], acc[:, dim:])
+        o = jnp.where(row1 % gb < half, acc[:, :dim], acc[:, dim:]) + p_new * v_new
         for h in range(heads):
-            o32[pl.ds(pl.multiple_of(g * gb, gb), gb), h * dim:(h + 1) * dim] = o[h * gb:(h + 1) * gb]
+            o32[mine, h * dim:(h + 1) * dim] = o[h * gb:(h + 1) * gb]
         for j in range(2):
-            copy_out(g, j).start()
+            bulk(g, j).wait()
+        for b8 in range(gb):
+            for j in range(2):
+                patch_copy(g * gb + b8, j).start()
 
     o_ref[...] = o32[...].astype(BF16)
-    for g in range(groups):
+
+    @pl.loop(0, rows)
+    def _(b):
         for j in range(2):
-            copy_out(g, j).wait()
-
-
-def mlp_kernel(nd, nt, fc, width_full, o_ref, hid_ref, gain_ref, wo_hbm, wg_hbm, wu_hbm, wd_hbm, out_ref,
-               wo, wg, wu, wd, o_all, acc32, rs1_s, rs1_r, mid, st_dm, st_tp, x2, gu_s, gu_r, gu_own, m_all,
+            patch_copy(b, j).wait()
+
+
+def mlp_kernel(nd, nt, fc, width_full, o_ref, hid_hbm, gain_hbm, wo_hbm, wg_hbm, wu_hbm, wd_hbm, out_ref,
+               hid_ref, gain_ref, wo, wg, wu, wd, o_all, acc32, rs1_s, rs1_r, mid, st_dm, st_tp, x2, gu_s, gu_r, gu_own, m_all,
                rs2_s, rs2_r, fin,
                wsem, o_ss, o_rs, a_ss, a_rs, b_ss, b_rs, sd_ss, sd_rs, st_ss, st_rs, g_ss, g_rs, m_ss, m_rs,
                c_ss, c_rs, d_ss, d_rs):
@@ -208,7 +221,9 @@
     wloads = [pltpu.make_async_copy(wo_hbm, wo, wsem.at[0]),
               pltpu.make_async_copy(wg_hbm, wg.at[pl.ds(0, ff)], wsem.at[1]),
               pltpu.make_async_copy(wu_hbm, wu.at[pl.ds(0, ff)], wsem.at[2]),
-              pltpu.make_async_copy(wd_hbm, wd.at[pl.ds(0, ff)], wsem.at[3])]
+              pltpu.make_async_copy(wd_hbm, wd.at[pl.ds(0, ff)], wsem.at[3]),
+              pltpu.make_async_copy(hid_hbm, hid_ref, wsem.at[4]),
+              pltpu.make_async_copy(gain_hbm, gain_ref, wsem.at[5])]
     for load in wloads:
         load.start()
     meet((('dm', nd), ('tp', nt)))
@@ -258,6 +273,8 @@
             sends.append(out[rel])
         return out
 
+    wloads[4].wait()
+    wloads[5].wait()
     attn = reduced(acc32, rs1_r, a_ss, a_rs, rs1_s)
     hid = hid_ref[pl.ds(pl.multiple_of(tp * rows_t, rows_t), rows_t), :]
     mine = (hid.astype(F32) + attn.astype(F32)).astype(BF16)
@@ -278,7 +295,7 @@
         total = total + st_dm[i]
     st_tp[tp] = total
     st_copies = gather(st_tp, st_ss, st_rs)
-    gain = gain_ref[...].astype(F32)
+    gain = gain_ref[...].astype(F32).reshape(1, width)
     for rel in range(nt):
         t = lax.rem(tp + nt - rel, nt)
         if rel:
@@ -342,6 +359,7 @@
 
 
 VMEM = pl.BlockSpec(memory_space=pltpu.VMEM)
+SEM = pl.BlockSpec(memory_space=pltpu.SEMAPHORE)
 SMEM = pl.BlockSpec(memory_space=pltpu.SMEM)
 HBM = pl.BlockSpec(memory_space=pltpu.HBM)
 MIB = 1 << 20
@@ -368,14 +386,23 @@
         def hbm(x):
             return pltpu.with_memory_space_constraint(x, pltpu.HBM)
 
+        def vmem(x):
+            return pltpu.with_memory_space_constraint(x, pltpu.VMEM)
+
+        flat = (rows, seq * heads, dim)
+        groups = rows // 8
         q, k, v = pl.pallas_call(
             functools.partial(qkv_kernel, nd, heads, width_full),
             out_shape=(jax.ShapeDtypeStruct((rows // 8, heads, 8, dim), F32),
                        jax.ShapeDtypeStruct((heads, rows, dim), F32),
                        jax.ShapeDtypeStruct((heads, rows, dim), F32)),
-            in_specs=[VMEM, VMEM, HBM, HBM, HBM, VMEM, VMEM],
+            in_specs=[HBM] * 7,
             out_specs=(VMEM, VMEM, VMEM),
             scratch_shapes=[
+                pltpu.VMEM((batch, width), BF16),
+                pltpu.VMEM((width,), BF16),
+                pltpu.VMEM(rope_cos.shape, F32),
+                pltpu.VMEM(rope_sin.shape, F32),
                 pltpu.VMEM((3, width * heads, dim), BF16),
                 pltpu.VMEM((width // 8 * heads, dim), F32),
                 pltpu.VMEM((3, width, cols), BF16),
@@ -383,32 +410,28 @@
                 pltpu.VMEM((3, nd, rows, cols), F32),
                 pltpu.VMEM((3, nd, rows, cols), BF16),
                 pltpu.VMEM((3, nd, rows, cols), BF16),
-                dma((3,)), dma((nd,)), dma((nd,)), dma((3, nd)), dma((3, nd)),
+                dma((4,)), dma((3,)), dma((nd,)), dma((nd,)), dma((3, nd)), dma((3, nd)),
             ],
             compiler_params=pltpu.CompilerParams(collective_id=0, has_side_effects=True, vmem_limit_bytes=16 * MIB),
+            cost_estimate=pl.CostEstimate(flops=10_000_000_000, bytes_accessed=32 * MIB, transcendentals=0),
             name='qkv',
-        )(hidden, norm_attn.reshape(1, width), hbm(w_q.reshape(width * heads, dim)), hbm(w_k.reshape(width * heads, dim)),
-          hbm(w_v.reshape(width * heads, dim)), rope_cos, rope_sin)
-
-        flat = (rows, seq * heads, dim)
+        )(hbm(hidden), hbm(norm_attn), hbm(w_q.reshape(width * heads, dim)), hbm(w_k.reshape(width * heads, dim)),
+          hbm(w_v.reshape(width * heads, dim)), hbm(rope_cos), hbm(rope_sin))
+
         o, k_new, v_new = pl.pallas_call(
             attend_kernel,
-            out_shape=(jax.ShapeDtypeStruct((rows, cols), BF16),
-                       jax.ShapeDtypeStruct(flat, BF16),
-                       jax.ShapeDtypeStruct(flat, BF16)),
-            in_specs=[SMEM, VMEM, VMEM, VMEM, HBM, HBM],
+            out_shape=(jax.ShapeDtypeStruct((rows, cols), BF16), jax.ShapeDtypeStruct(flat, BF16), jax.ShapeDtypeStruct(flat, BF16)),
+            in_specs=[SMEM, VMEM, VMEM, VMEM, VMEM, VMEM],
             out_specs=(VMEM, HBM, HBM),
             scratch_shapes=[
-                pltpu.VMEM(flat, BF16),
-                pltpu.VMEM(flat, BF16),
-                pltpu.VMEM((rows * 16, dim), F32),
-                pltpu.VMEM((2, rows * 16, dim), BF16),
+                pltpu.VMEM((2, rows * 16, dim), F32),
+                pltpu.VMEM((2, rows, 16, dim), BF16),
                 pltpu.VMEM((rows, cols), F32),
-                dma((2, rows // 8)), dma((2, rows // 8)),
+                dma((2, rows // 8)), dma((2, rows)),
             ],
-            compiler_params=pltpu.CompilerParams(vmem_limit_bytes=40 * MIB),
+            compiler_params=pltpu.CompilerParams(vmem_limit_bytes=8 * MIB),
             name='attend',
-        )(seq_lens, q, k, v, hbm(k_cache.reshape(flat)), hbm(v_cache.reshape(flat)))
+        )(seq_lens, q, k, v, vmem(k_cache.reshape(flat)), vmem(v_cache.reshape(flat)))
 
         fc = -(-ff // (nd * 16)) * 16
         rows_t = batch // nt
@@ -416,9 +439,11 @@
         out = pl.pallas_call(
             functools.partial(mlp_kernel, nd, nt, fc, width_full),
             out_shape=jax.ShapeDtypeStruct((batch, width), BF16),
-            in_specs=[VMEM, VMEM, VMEM, HBM, HBM, HBM, HBM],
+            in_specs=[VMEM] + [HBM] * 6,
             out_specs=VMEM,
             scratch_shapes=[
+                pltpu.VMEM((batch, width), BF16),
+                pltpu.VMEM((width,), BF16),
                 pltpu.VMEM((cols, width), BF16),
                 pltpu.VMEM((nd * fc, width), BF16),
                 pltpu.VMEM((nd * fc, width), BF16),
@@ -438,13 +463,13 @@
                 pltpu.VMEM(slab, BF16),
                 pltpu.VMEM(slab, BF16),
                 pltpu.VMEM(slab, BF16),
-                dma((4,)), dma((nd,)), dma((nd,)), dma((nt,)), dma((nt,)), dma((nt,)), dma((nt,)),
+                dma((6,)), dma((nd,)), dma((nd,)), dma((nt,)), dma((nt,)), dma((nt,)), dma((nt,)),
                 dma((nd,)), dma((nd,)), dma((nt,)), dma((nt,)), dma((nd,)), dma((nd,)), dma((nd,)), dma((nd,)),
                 dma((nt,)), dma((nt,)), dma((nt,)), dma((nt,)),
             ],
             compiler_params=pltpu.CompilerParams(collective_id=1, has_side_effects=True, vmem_limit_bytes=24 * MIB),
             name='mlp',
-        )(o, hidden, norm_mlp.reshape(1, width), hbm(w_o.reshape(cols, width)), hbm(w_gate.T), hbm(w_up.T), hbm(w_down))
+        )(o, hbm(hidden), hbm(norm_mlp), hbm(w_o.reshape(cols, width)), hbm(w_gate.T), hbm(w_up.T), hbm(w_down))
         return out, k_new.reshape(k_cache.shape), v_new.reshape(v_cache.shape)
 
     return jax.shard_map(local_layer, mesh=mesh, in_specs=in_specs, out_specs=out_specs, check_vma=False)

time: 84.1 us -> 77.2 us (0.918)
  local copies, waits for them, and re-layouts: 5.11 us -> 0.72 us
  Pallas kernels: 78 us -> 75.7 us
    pallas_call x1, Pallas kernels: 13.4 us -> 9.48 us  [local_layer(): pl.pallas_call(attend_kernel, out_shape=(jax.ShapeDtypeStruct((rows, cols...]
    unnamed x11 -> x7, local copies, waits for them, and re-layouts: 3.74 us -> 0.72 us
    pallas_call x1, Pallas kernels: 13.9 us -> 15.6 us  [local_layer(): pl.pallas_call(functools.partial(qkv_kernel, nd, heads, width_full), out_...]
    reshape x2 -> x0, local copies, waits for them, and re-layouts: 1.37 us -> none  [the longest x1 0.69 us: local_layer(): norm_attn.reshape(1, width)]
where the time goes in v2:
time: 77.2 us; the launch traced here: 77.1 us
  Pallas kernels  75.7 us (98%)
    pallas_call x1, Pallas kernels, local_layer(): pl.pallas_call(functools.partial(mlp_kernel, nd, nt, fc, width_full), out...  50.7 us
    pallas_call x1, Pallas kernels, local_layer(): pl.pallas_call(functools.partial(qkv_kernel, nd, heads, width_full), out_...  15.6 us
    pallas_call x1, Pallas kernels, local_layer(): pl.pallas_call(attend_kernel, out_shape=(jax.ShapeDtypeStruct((rows, cols...  9.48 us

profile of v2, /device:TPU:97, one launch (start us, length us, event | category | flops | bytes accessed | tf_op | source)
XLA Modules:
  0.0 77.1 jit_solution(2050053447997400757)
XLA Ops:
  0.6 0.0 copy-start
  0.6 0.0 copy-start.1
  0.7 0.0 copy-start.2
  0.7 15.6 %qkv.1 = (f32[4,4,8,128]{3,2,1,0:T(8,128)S(1)}, f32[4,32,128]{2,1,0:T(8,128)S(1)}, f32[4,32,128]{2,1,0:T(8,128)S(1)}) custom-call(bf16[128,1024]{1,0:T(8,128)(2,1)} %hid_hbm.3, bf16[1024]{0:T(1024)(128)(2,1)} %gain_hbm.2, bf16[4096,128]{1,0:T(8,128)(2,1)} %bitcast.17, bf16[4096,128]{1,0:T(8,128)(2,1)} %bitcast.18, bf16[4096,128]{1,0:T(8,128)(2,1)} %bitcast.19, ...), custom_call_target="tpu_custom_call" | custom-call | flops 10000000000 | bytes 33554432 | tf_op jit(solution)/shard_map/qkv/pallas_call | solution.py:394
  16.2 0.0 copy-done
  16.2 0.0 copy-done.1
  16.2 0.0 copy-done.2
  16.3 9.5 %attend.1 = (bf16[32,512]{1,0:T(8,128)(2,1)S(1)}, bf16[32,1024,128]{2,1,0:T(8,128)(2,1)}, bf16[32,1024,128]{2,1,0:T(8,128)(2,1)}) custom-call(s32[32]{0:T(128)S(1)} %copy-done.2, f32[4,4,8,128]{3,2,1,0:T(8,128)S(1)} %get-tuple-element.9.q_ref, f32[4,32,128]{2,1,0:T(8,128)S(1)} %get-tuple-element.10.knew_ref, f32[4,32,128]{2,1,0:T(8,128)S(1)} %get-tuple-element.11.vnew_ref, ...), custom_call_target="tpu_custom_call" | custom-call | tf_op jit(solution)/shard_map/attend/pallas_call | solution.py:421
  25.7 50.7 %mlp.1 = bf16[128,1024]{1,0:T(8,128)(2,1)S(1)} custom-call(bf16[32,512]{1,0:T(8,128)(2,1)S(1)} %get-tuple-element.12.o_ref, bf16[128,1024]{1,0:T(8,128)(2,1)} %hid_hbm.3, bf16[1024]{0:T(1024)(128)(2,1)} %gain_hbm.3, bf16[512,1024]{1,0:T(8,128)(2,1)} %bitcast.14, bf16[1376,1024]{1,0:T(8,128)(2,1)} %bitcast.12, bf16[1376,1024]{1,0:T(8,128)(2,1)} %bitcast.13, ...), custom_call_target="tpu_custom_call" | custom-call | tf_op jit(solution)/shard_map/mlp/pallas_call | solution.py:439
  76.4 0.7 copy.19
Async XLA Ops:
  0.6 15.6 %copy-start = (bf16[32,256,4,128]{3,2,1,0:T(4,128)(2,1)S(1)}, bf16[32,256,4,128]{3,2,1,0:T(4,128)(2,1)}, u32[]{:S(2)}) copy-start(bf16[32,256,4,128]{3,2,1,0:T(4,128)(2,1)} %param.25) | copy-start | bytes 25165828
  0.6 15.6 %copy-start.1 = (bf16[32,256,4,128]{3,2,1,0:T(4,128)(2,1)S(1)}, bf16[32,256,4,128]{3,2,1,0:T(4,128)(2,1)}, u32[]{:S(2)}) copy-start(bf16[32,256,4,128]{3,2,1,0:T(4,128)(2,1)} %param.26) | copy-start | bytes 25165828
  0.7 15.6 %copy-start.2 = (s32[32]{0:T(128)S(1)}, s32[32]{0:T(128)}, u32[]{:S(2)}) copy-start(s32[32]{0:T(128)} %len_ref.1) | copy-start | bytes 388

commit v3 on v2

--- a/solution.py
+++ b/solution.py
@@ -48,7 +48,7 @@
 
 def qkv_kernel(nd, heads, width_full, hid_hbm, gain_hbm, wq_ref, wk_ref, wv_ref, cos_hbm, sin_hbm,
                q_out, k_out, v_out,
-               hid_ref, gain_ref, cos_ref, sin_ref, wbuf, w32, wcat, stat, part, sbuf, rbuf,
+               hid_ref, gain_ref, cos_ref, sin_ref, wbuf, w32, wcat, order, stat, part, sbuf, rbuf,
                isem, wsem, st_ss, st_rs, ss, rs):
     me = lax.axis_index('dm')
     batch, width = hid_ref.shape
@@ -115,101 +115,60 @@
             v = v.astype(BF16).astype(F32)
             if j == 0:
                 q_out[:, h] = v.reshape(rows // 8, 8, 128)
-            elif j == 1:
-                k_out[h] = v
             else:
-                v_out[h] = v
+                order[pl.ds(h, rows, stride=heads), :] = v
+        if j:
+            (k_out, v_out)[j - 1][...] = order[...].astype(BF16)
     for copy in copies:
         copy.wait_send()
 
 
-def attend_kernel(len_ref, q_ref, knew_ref, vnew_ref, k_buf, v_buf, o_ref, k_out, v_out, new, patch, o32, out_sem, patch_sem):
+def attend_kernel(len_ref, q_ref, k_buf, v_buf, o_ref, o32):
     groups, heads, gb, dim = q_ref.shape
     rows, span, _ = k_buf.shape
-    per = 16 // heads
-    caches = ((k_buf, k_out), (v_buf, v_out))
-
-    def bulk(g, j):
-        at = pl.ds(g * gb, gb)
-        return pltpu.make_async_copy(caches[j][0].at[at], caches[j][1].at[at], out_sem.at[j, g])
-
-    def patch_copy(b, j):
-        at = pl.ds(pl.multiple_of((len_ref[b] // per) * 16, 16), 16)
-        return pltpu.make_async_copy(patch.at[j, b], caches[j][1].at[b, at], patch_sem.at[j, b])
-
-    for g in range(groups):
-        for j in range(2):
-            bulk(g, j).start()
     lane = lax.broadcasted_iota(jnp.int32, (heads * gb, span), 1)
     row = lax.broadcasted_iota(jnp.int32, (heads * gb, span), 0)
     head_ok = lane % heads == row // gb
     slot = lane // heads
     row1 = lax.broadcasted_iota(jnp.int32, (heads * gb, dim), 0)
-    r16 = lax.broadcasted_iota(jnp.int32, (16, dim), 0) // heads
-    for j, src in enumerate((knew_ref, vnew_ref)):
-        for h in range(heads):
-            for s in range(per):
-                new[j, pl.ds(s * heads + h, rows, stride=16), :] = src[h]
 
     @pl.loop(0, groups)
     def _(g):
         lens = jnp.zeros((heads * gb, dim), jnp.int32)
         for b8 in range(gb):
-            b = g * gb + b8
-            n = len_ref[b]
-            lens = jnp.where(row1 % gb == b8, n, lens)
-            at = pl.ds(pl.multiple_of((n // per) * 16, 16), 16)
-            src = pl.ds(pl.multiple_of(b * 16, 16), 16)
-            for j in range(2):
-                old = caches[j][0][b, at, :].astype(F32)
-                patch[j, b] = jnp.where(r16 == n % per, new[j, src, :], old).astype(BF16)
+            lens = jnp.where(row1 % gb == b8, len_ref[g * gb + b8], lens)
         mine = pl.ds(pl.multiple_of(g * gb, gb), gb)
         q = jnp.concatenate([q_ref[g, h] for h in range(heads)], axis=0)
-        k_new = jnp.concatenate([knew_ref[h, mine, :] for h in range(heads)], axis=0)
-        v_new = jnp.concatenate([vnew_ref[h, mine, :] for h in range(heads)], axis=0)
         q_exp = jnp.concatenate([jnp.where(row1 % gb == b8, q, 0.0).astype(BF16) for b8 in range(gb)], axis=1)
         parts = []
         for nb in range(span // 256):
             keys = jnp.concatenate([k_buf[g * gb + b8, nb * 256:(nb + 1) * 256, :] for b8 in range(gb)], axis=1)
             parts.append(lax.dot_general(q_exp, keys, NT_DIMS, preferred_element_type=F32))
         s = jnp.concatenate(parts, axis=1) * (dim ** -0.5)
-        s_new = jnp.sum(q * k_new, axis=1, keepdims=True) * (dim ** -0.5)
-        ok = head_ok & (slot < jnp.concatenate([lens] * (span // dim), axis=1))
+        ok = head_ok & (slot <= jnp.concatenate([lens] * (span // dim), axis=1))
         s = jnp.where(ok, s, -1e30)
-        top = jnp.maximum(jnp.max(s, axis=1, keepdims=True), s_new)
+        top = jnp.max(s, axis=1, keepdims=True)
         e = jnp.where(ok, jnp.exp(s - top), 0.0)
-        e_new = jnp.exp(s_new - top)
-        total = jnp.sum(e, axis=1, keepdims=True) + e_new
-        p = e / total
-        p_new = (e_new / total).astype(BF16).astype(F32)
+        p = e / jnp.sum(e, axis=1, keepdims=True)
         acc = jnp.zeros((heads * gb, 2 * dim), F32)
         half = gb // 2
         for pair in range(half):
             p_pair = jnp.where(row % half == pair, p, 0.0).astype(BF16)
             vals = jnp.concatenate([v_buf[g * gb + pair], v_buf[g * gb + pair + half]], axis=1)
             acc = acc + jnp.dot(p_pair, vals, preferred_element_type=F32)
-        o = jnp.where(row1 % gb < half, acc[:, :dim], acc[:, dim:]) + p_new * v_new
+        o = jnp.where(row1 % gb < half, acc[:, :dim], acc[:, dim:])
         for h in range(heads):
             o32[mine, h * dim:(h + 1) * dim] = o[h * gb:(h + 1) * gb]
-        for j in range(2):
-            bulk(g, j).wait()
-        for b8 in range(gb):
-            for j in range(2):
-                patch_copy(g * gb + b8, j).start()
 
     o_ref[...] = o32[...].astype(BF16)
 
-    @pl.loop(0, rows)
-    def _(b):
-        for j in range(2):
-            patch_copy(b, j).wait()
-
-
-def mlp_kernel(nd, nt, fc, width_full, o_ref, hid_hbm, gain_hbm, wo_hbm, wg_hbm, wu_hbm, wd_hbm, out_ref,
+
+def mlp_kernel(nd, nt, fc, width_full, o_ref, hid_hbm, gain_hbm, wo_hbm, wg_hbm, wu_hbm, wd_hbm, k_kept, v_kept, out_ref,
                hid_ref, gain_ref, wo, wg, wu, wd, o_all, acc32, rs1_s, rs1_r, mid, st_dm, st_tp, x2, gu_s, gu_r, gu_own, m_all,
                rs2_s, rs2_r, fin,
                wsem, o_ss, o_rs, a_ss, a_rs, b_ss, b_rs, sd_ss, sd_rs, st_ss, st_rs, g_ss, g_rs, m_ss, m_rs,
                c_ss, c_rs, d_ss, d_rs):
+    del k_kept, v_kept
     dm = lax.axis_index('dm')
     tp = lax.axis_index('tp')
     rows_d = o_ref.shape[0]
@@ -394,8 +353,8 @@
         q, k, v = pl.pallas_call(
             functools.partial(qkv_kernel, nd, heads, width_full),
             out_shape=(jax.ShapeDtypeStruct((rows // 8, heads, 8, dim), F32),
-                       jax.ShapeDtypeStruct((heads, rows, dim), F32),
-                       jax.ShapeDtypeStruct((heads, rows, dim), F32)),
+                       jax.ShapeDtypeStruct((rows * heads, dim), BF16),
+                       jax.ShapeDtypeStruct((rows * heads, dim), BF16)),
             in_specs=[HBM] * 7,
             out_specs=(VMEM, VMEM, VMEM),
             scratch_shapes=[
@@ -406,6 +365,7 @@
                 pltpu.VMEM((3, width * heads, dim), BF16),
                 pltpu.VMEM((width // 8 * heads, dim), F32),
                 pltpu.VMEM((3, width, cols), BF16),
+                pltpu.VMEM((rows * heads, dim), F32),
                 pltpu.VMEM((nd, 1, batch), F32),
                 pltpu.VMEM((3, nd, rows, cols), F32),
                 pltpu.VMEM((3, nd, rows, cols), BF16),
@@ -418,20 +378,22 @@
         )(hbm(hidden), hbm(norm_attn), hbm(w_q.reshape(width * heads, dim)), hbm(w_k.reshape(width * heads, dim)),
           hbm(w_v.reshape(width * heads, dim)), hbm(rope_cos), hbm(rope_sin))
 
-        o, k_new, v_new = pl.pallas_call(
+        hit = (jnp.arange(seq)[None, :] == seq_lens[:, None])[:, :, None, None]
+        k_new = jnp.where(hit, k.reshape(rows, 1, heads, dim), k_cache)
+        v_new = jnp.where(hit, v.reshape(rows, 1, heads, dim), v_cache)
+        k_kept = vmem(k_new.reshape(flat))
+        v_kept = vmem(v_new.reshape(flat))
+        o = pl.pallas_call(
             attend_kernel,
-            out_shape=(jax.ShapeDtypeStruct((rows, cols), BF16), jax.ShapeDtypeStruct(flat, BF16), jax.ShapeDtypeStruct(flat, BF16)),
-            in_specs=[SMEM, VMEM, VMEM, VMEM, VMEM, VMEM],
-            out_specs=(VMEM, HBM, HBM),
+            out_shape=jax.ShapeDtypeStruct((rows, cols), BF16),
+            in_specs=[SMEM, VMEM, VMEM, VMEM],
+            out_specs=VMEM,
             scratch_shapes=[
-                pltpu.VMEM((2, rows * 16, dim), F32),
-                pltpu.VMEM((2, rows, 16, dim), BF16),
                 pltpu.VMEM((rows, cols), F32),
-                dma((2, rows // 8)), dma((2, rows)),
             ],
             compiler_params=pltpu.CompilerParams(vmem_limit_bytes=8 * MIB),
             name='attend',
-        )(seq_lens, q, k, v, vmem(k_cache.reshape(flat)), vmem(v_cache.reshape(flat)))
+        )(seq_lens, q, k_kept, v_kept)
 
         fc = -(-ff // (nd * 16)) * 16
         rows_t = batch // nt
@@ -439,7 +401,7 @@
         out = pl.pallas_call(
             functools.partial(mlp_kernel, nd, nt, fc, width_full),
             out_shape=jax.ShapeDtypeStruct((batch, width), BF16),
-            in_specs=[VMEM] + [HBM] * 6,
+            in_specs=[VMEM] + [HBM] * 6 + [VMEM, VMEM],
             out_specs=VMEM,
             scratch_shapes=[
                 pltpu.VMEM((batch, width), BF16),
@@ -468,8 +430,9 @@
                 dma((nt,)), dma((nt,)), dma((nt,)), dma((nt,)),
             ],
             compiler_params=pltpu.CompilerParams(collective_id=1, has_side_effects=True, vmem_limit_bytes=24 * MIB),
+            cost_estimate=pl.CostEstimate(flops=40_000_000_000, bytes_accessed=12 * MIB, transcendentals=0),
             name='mlp',
-        )(o, hbm(hidden), hbm(norm_mlp), hbm(w_o.reshape(cols, width)), hbm(w_gate.T), hbm(w_up.T), hbm(w_down))
+        )(o, hbm(hidden), hbm(norm_mlp), hbm(w_o.reshape(cols, width)), hbm(w_gate.T), hbm(w_up.T), hbm(w_down), k_kept, v_kept)
         return out, k_new.reshape(k_cache.shape), v_new.reshape(v_cache.shape)
 
     return jax.shard_map(local_layer, mesh=mesh, in_specs=in_specs, out_specs=out_specs, check_vma=False)

time: 77.2 us -> 87.9 us (1.14)
  other arithmetic: 0 us -> 12.4 us
  Pallas kernels: 75.7 us -> 73.9 us
    select_n x0 -> x1, other arithmetic: none -> 11.7 us  [local_layer(): v_new = jnp.where(hit, v.reshape(rows, 1, heads, dim), v_cache)]
    pallas_call x1, Pallas kernels: 9.48 us -> 7.64 us  [local_layer(): pl.pallas_call(attend_kernel, out_shape=jax.ShapeDtypeStruct((rows, cols)...]
where the time goes in v3:
time: 87.9 us; the launch traced here: 87.8 us
  Pallas kernels  73.9 us (84%)
  other arithmetic  12.4 us (14%)
    pallas_call x1, Pallas kernels, local_layer(): pl.pallas_call(functools.partial(mlp_kernel, nd, nt, fc, width_full), out...  50.7 us
    pallas_call x1, Pallas kernels, local_layer(): pl.pallas_call(functools.partial(qkv_kernel, nd, heads, width_full), out_...  15.6 us
    select_n x1, other arithmetic, local_layer(): v_new = jnp.where(hit, v.reshape(rows, 1, heads, dim), v_cache)  11.7 us
    pallas_call x1, Pallas kernels, local_layer(): pl.pallas_call(attend_kernel, out_shape=jax.ShapeDtypeStruct((rows, cols)...  7.64 us

profile of v3, /device:TPU:97, one launch (start us, length us, event | category | flops | bytes accessed | tf_op | source)
XLA Modules:
  0.0 87.8 jit_solution(4639872133562276901)
XLA Ops:
  0.6 0.7 iota_compare_fusion
  1.4 0.0 copy-start.3
  1.4 0.0 copy-start.4
  1.4 15.6 %qkv.1 = (f32[4,4,8,128]{3,2,1,0:T(8,128)S(1)}, bf16[128,128]{1,0:T(8,128)(2,1)S(1)}, bf16[128,128]{1,0:T(8,128)(2,1)S(1)}) custom-call(bf16[128,1024]{1,0:T(8,128)(2,1)} %hid_hbm.3, bf16[1024]{0:T(1024)(128)(2,1)} %gain_hbm.2, bf16[4096,128]{1,0:T(8,128)(2,1)} %bitcast.18, bf16[4096,128]{1,0:T(8,128)(2,1)} %bitcast.19, bf16[4096,128]{1,0:T(8,128)(2,1)} %bitcast.20, ...), custom_call_target="tpu_custom_call" | custom-call | flops 10000000000 | bytes 33554432 | tf_op jit(solution)/shard_map/qkv/pallas_call | solution.py:353
  16.9 0.0 copy-done.3
  17.0 0.0 copy-done.4
  17.0 0.0 copy-start.2
  17.0 11.7 %broadcast_select_fusion = (bf16[32,256,4,128]{3,2,1,0:T(4,128)(2,1)S(1)}, bf16[32,256,4,128]{3,2,1,0:T(4,128)(2,1)S(1)}) fusion(bf16[32,256,4,128]{3,2,1,0:T(4,128)(2,1)S(1)} %copy-done.3, pred[32,256]{1,0:T(8,128)(4,1)S(1)} %iota_compare_fusion, bf16[32,4,128]{2,1,0:T(4,128)(2,1)S(1)} %bitcast.15, bf16[32,256,4,128]{3,2,1,0:T(4,128)(2,1)S(1)} %copy-done.4, ...), kind=kLoop, calls=%fused_computation | loop fusion | flops 8388608 | bytes 33628160 | tf_op jit(solution)/shard_map/jit(_where)/select_n | solution.py:383
  28.6 0.0 copy-start
  28.7 0.0 copy-start.1
  28.7 0.0 copy-done.2
  28.7 7.6 %attend.1.o_ref = bf16[32,512]{1,0:T(8,128)(2,1)S(1)} custom-call(s32[32]{0:T(128)S(1)} %copy-done.2, f32[4,4,8,128]{3,2,1,0:T(8,128)S(1)} %get-tuple-element.6.q_ref, bf16[32,1024,128]{2,1,0:T(8,128)(2,1)S(1)} %bitcast.12, bf16[32,1024,128]{2,1,0:T(8,128)(2,1)S(1)} %bitcast.10), custom_call_target="tpu_custom_call" | custom-call | tf_op jit(solution)/shard_map/attend/pallas_call | solution.py:386
  36.3 0.0 copy-done
  36.3 0.0 copy-done.1
  36.3 50.7 %mlp.1 = bf16[128,1024]{1,0:T(8,128)(2,1)S(1)} custom-call(bf16[32,512]{1,0:T(8,128)(2,1)S(1)} %attend.1.o_ref, bf16[128,1024]{1,0:T(8,128)(2,1)} %hid_hbm.3, bf16[1024]{0:T(1024)(128)(2,1)} %gain_hbm.3, bf16[512,1024]{1,0:T(8,128)(2,1)} %bitcast.21, bf16[1376,1024]{1,0:T(8,128)(2,1)} %bitcast.16, bf16[1376,1024]{1,0:T(8,128)(2,1)} %bitcast.17, ...), custom_call_target="tpu_custom_call" | custom-call | flops 40000000000 | bytes 12582912 | tf_op jit(solution)/shard_map/mlp/pallas_call | solution.py:401
  87.1 0.7 copy.19
Async XLA Ops:
  1.4 15.6 %copy-start.3 = (bf16[32,256,4,128]{3,2,1,0:T(4,128)(2,1)S(1)}, bf16[32,256,4,128]{3,2,1,0:T(4,128)(2,1)}, u32[]{:S(2)}) copy-start(bf16[32,256,4,128]{3,2,1,0:T(4,128)(2,1)} %param.26) | copy-start | bytes 25165828
  1.4 15.6 %copy-start.4 = (bf16[32,256,4,128]{3,2,1,0:T(4,128)(2,1)S(1)}, bf16[32,256,4,128]{3,2,1,0:T(4,128)(2,1)}, u32[]{:S(2)}) copy-start(bf16[32,256,4,128]{3,2,1,0:T(4,128)(2,1)} %param.25) | copy-start | bytes 25165828
  17.0 11.7 %copy-start.2 = (s32[32]{0:T(128)S(1)}, s32[32]{0:T(128)}, u32[]{:S(2)}) copy-start(s32[32]{0:T(128)} %len_ref.1) | copy-start | bytes 388
  28.6 7.7 %copy-start = (bf16[32,256,4,128]{3,2,1,0:T(4,128)(2,1)}, bf16[32,256,4,128]{3,2,1,0:T(4,128)(2,1)S(1)}, u32[]{:S(2)}) copy-start(bf16[32,256,4,128]{3,2,1,0:T(4,128)(2,1)S(1)} %get-tuple-element.16) | copy-start | bytes 25165828
  28.7 7.7 %copy-start.1 = (bf16[32,256,4,128]{3,2,1,0:T(4,128)(2,1)}, bf16[32,256,4,128]{3,2,1,0:T(4,128)(2,1)S(1)}, u32[]{:S(2)}) copy-start(bf16[32,256,4,128]{3,2,1,0:T(4,128)(2,1)S(1)} %get-tuple-element.15) | copy-start | bytes 25165828

commit v4 on v2

--- a/solution.py
+++ b/solution.py
@@ -191,13 +191,15 @@
         o = jnp.where(row1 % gb < half, acc[:, :dim], acc[:, dim:]) + p_new * v_new
         for h in range(heads):
             o32[mine, h * dim:(h + 1) * dim] = o[h * gb:(h + 1) * gb]
+
+    o_ref[...] = o32[...].astype(BF16)
+
+    @pl.loop(0, groups)
+    def _(g):
         for j in range(2):
             bulk(g, j).wait()
-        for b8 in range(gb):
-            for j in range(2):
+            for b8 in range(gb):
                 patch_copy(g * gb + b8, j).start()
-
-    o_ref[...] = o32[...].astype(BF16)
 
     @pl.loop(0, rows)
     def _(b):
@@ -206,7 +208,7 @@
 
 
 def mlp_kernel(nd, nt, fc, width_full, o_ref, hid_hbm, gain_hbm, wo_hbm, wg_hbm, wu_hbm, wd_hbm, out_ref,
-               hid_ref, gain_ref, wo, wg, wu, wd, o_all, acc32, rs1_s, rs1_r, mid, st_dm, st_tp, x2, gu_s, gu_r, gu_own, m_all,
+               hid_ref, gain_ref, wo, wg, wu, wd, o_all, acc32, rs1_s, rs1_r, mid, st_dm, st_tp, x2, gu_far, gu_relay, gu_s, gu_r, gu_own, m_all,
                rs2_s, rs2_r, fin,
                wsem, o_ss, o_rs, a_ss, a_rs, b_ss, b_rs, sd_ss, sd_rs, st_ss, st_rs, g_ss, g_rs, m_ss, m_rs,
                c_ss, c_rs, d_ss, d_rs):
@@ -305,27 +307,42 @@
         x2[pl.ds(pl.multiple_of(t * rows_t, rows_t), rows_t), :] = (mid[t].astype(F32) * scale * gain).astype(BF16)
     wloads[1].wait()
     wloads[2].wait()
-    g_copies = {}
-    for rel in (2, 1, 3, 0) if nd == 4 else [*range(1, nd), 0]:
-        to = lax.rem(dm + rel, nd)
-        at = pl.ds(pl.multiple_of(to * fc, 16), fc)
-        for i, w in enumerate((wg, wu)):
-            part = lax.dot_general(w[at, :], x2[...], NT_DIMS, preferred_element_type=F32)
-            if rel:
-                gu_s[to, i] = part.astype(BF16)
-            else:
-                gu_own[i] = part
-        if rel:
-            g_copies[rel] = remote(gu_s.at[to], gu_r.at[dm], g_ss.at[rel], g_rs.at[rel], 'dm', to)
-            g_copies[rel].start()
-            sends.append(g_copies[rel])
-    gate = gu_own[0]
-    up = gu_own[1]
-    for rel in (1, 3, 2) if nd == 4 else range(1, nd):
-        frm = lax.rem(dm + nd - rel, nd)
-        g_copies[rel].wait_recv()
-        gate = gate + gu_r[frm, 0].astype(F32)
-        up = up + gu_r[frm, 1].astype(F32)
+    half = fc // 2
+    left, right, far = (lax.rem(dm + i, nd) for i in (nd - 1, 1, 2))
+
+    def gate_up(to, h):
+        at = pl.ds(pl.multiple_of(to * fc + h * half, 16), half)
+        both = jnp.concatenate([wg[at, :], wu[at, :]], axis=0)
+        return lax.dot_general(both, x2[...], NT_DIMS, preferred_element_type=F32)
+
+    def send(src, dst, k, to):
+        copy = remote(src, dst, g_ss.at[k], g_rs.at[k], 'dm', to)
+        copy.start()
+        sends.append(copy)
+        return copy
+
+    steps = ((right, 0), (left, 1))
+    relays = []
+    for to, h in steps:
+        gu_far[h] = gate_up(far, h).astype(BF16)
+        relays.append(send(gu_far.at[h], gu_relay.at[h], h, to))
+    arrived = []
+    for to, h in steps:
+        gu_s[h, 1 - h] = gate_up(to, 1 - h).astype(BF16)
+        arrived.append(send(gu_s.at[h, 1 - h], gu_r.at[h, 1 - h], 2 + h, to))
+    for to, h in steps:
+        gu_own[2 + h] = gate_up(to, h)
+    for h in range(2):
+        gu_own[h] = gate_up(dm, h)
+    for to, h in steps:
+        relays[h].wait_recv()
+        gu_s[h, h] = (gu_own[2 + h] + gu_relay[h].astype(F32)).astype(BF16)
+        arrived.append(send(gu_s.at[h, h], gu_r.at[h, h], 4 + h, to))
+    for copy in arrived:
+        copy.wait_recv()
+    sums = [gu_own[h] + gu_r[0, h].astype(F32) + gu_r[1, h].astype(F32) for h in range(2)]
+    gate = jnp.concatenate([x[:half] for x in sums], axis=0)
+    up = jnp.concatenate([x[half:] for x in sums], axis=0)
     m_all[dm] = (gate / (1.0 + jnp.exp(-gate)) * up).astype(BF16)
     m_copies = {}
     for rel in (2, 1, 3) if nd == 4 else range(1, nd):
@@ -433,7 +450,7 @@
             name='attend',
         )(seq_lens, q, k, v, vmem(k_cache.reshape(flat)), vmem(v_cache.reshape(flat)))
 
-        fc = -(-ff // (nd * 16)) * 16
+        fc = -(-ff // (nd * 32)) * 32
         rows_t = batch // nt
         slab = (nt, rows_t, width)
         out = pl.pallas_call(
@@ -456,15 +473,17 @@
                 pltpu.VMEM((nd, 1, 128), F32),
                 pltpu.VMEM((nt, 1, 128), F32),
                 pltpu.VMEM((batch, width), BF16),
-                pltpu.VMEM((nd, 2, fc, batch), BF16),
-                pltpu.VMEM((nd, 2, fc, batch), BF16),
-                pltpu.VMEM((2, fc, batch), F32),
+                pltpu.VMEM((2, fc, batch), BF16),
+                pltpu.VMEM((2, fc, batch), BF16),
+                pltpu.VMEM((2, 2, fc, batch), BF16),
+                pltpu.VMEM((2, 2, fc, batch), BF16),
+                pltpu.VMEM((4, fc, batch), F32),
                 pltpu.VMEM((nd, fc, batch), BF16),
                 pltpu.VMEM(slab, BF16),
                 pltpu.VMEM(slab, BF16),
                 pltpu.VMEM(slab, BF16),
                 dma((6,)), dma((nd,)), dma((nd,)), dma((nt,)), dma((nt,)), dma((nt,)), dma((nt,)),
-                dma((nd,)), dma((nd,)), dma((nt,)), dma((nt,)), dma((nd,)), dma((nd,)), dma((nd,)), dma((nd,)),
+                dma((nd,)), dma((nd,)), dma((nt,)), dma((nt,)), dma((6,)), dma((6,)), dma((nd,)), dma((nd,)),
                 dma((nt,)), dma((nt,)), dma((nt,)), dma((nt,)),
             ],
             compiler_params=pltpu.CompilerParams(collective_id=1, has_side_effects=True, vmem_limit_bytes=24 * MIB),

time: 77.2 us -> 75.4 us (0.977)
  Pallas kernels: 75.7 us -> 73.9 us
    pallas_call x1, Pallas kernels: 50.7 us -> 48.8 us  [local_layer(): pl.pallas_call(functools.partial(mlp_kernel, nd, nt, fc, width_full), out...]
where the time goes in v4:
time: 75.4 us; the launch traced here: 75.3 us
  Pallas kernels  73.9 us (98%)
    pallas_call x1, Pallas kernels, local_layer(): pl.pallas_call(functools.partial(mlp_kernel, nd, nt, fc, width_full), out...  48.8 us
    pallas_call x1, Pallas kernels, local_layer(): pl.pallas_call(functools.partial(qkv_kernel, nd, heads, width_full), out_...  15.6 us
    pallas_call x1, Pallas kernels, local_layer(): pl.pallas_call(attend_kernel, out_shape=(jax.ShapeDtypeStruct((rows, cols...  9.59 us

profile of v4, /device:TPU:97, one launch (start us, length us, event | category | flops | bytes accessed | tf_op | source)
XLA Modules:
  0.0 75.3 jit_solution(8922875943288981689)
XLA Ops:
  0.6 0.0 copy-start
  0.6 0.0 copy-start.1
  0.7 0.0 copy-start.2
  0.7 15.6 %qkv.1 = (f32[4,4,8,128]{3,2,1,0:T(8,128)S(1)}, f32[4,32,128]{2,1,0:T(8,128)S(1)}, f32[4,32,128]{2,1,0:T(8,128)S(1)}) custom-call(bf16[128,1024]{1,0:T(8,128)(2,1)} %hid_hbm.3, bf16[1024]{0:T(1024)(128)(2,1)} %gain_hbm.2, bf16[4096,128]{1,0:T(8,128)(2,1)} %bitcast.17, bf16[4096,128]{1,0:T(8,128)(2,1)} %bitcast.18, bf16[4096,128]{1,0:T(8,128)(2,1)} %bitcast.19, ...), custom_call_target="tpu_custom_call" | custom-call | flops 10000000000 | bytes 33554432 | tf_op jit(solution)/shard_map/qkv/pallas_call | solution.py:411
  16.2 0.0 copy-done
  16.2 0.0 copy-done.1
  16.2 0.0 copy-done.2
  16.3 9.6 %attend.1 = (bf16[32,512]{1,0:T(8,128)(2,1)S(1)}, bf16[32,1024,128]{2,1,0:T(8,128)(2,1)}, bf16[32,1024,128]{2,1,0:T(8,128)(2,1)}) custom-call(s32[32]{0:T(128)S(1)} %copy-done.2, f32[4,4,8,128]{3,2,1,0:T(8,128)S(1)} %get-tuple-element.9.q_ref, f32[4,32,128]{2,1,0:T(8,128)S(1)} %get-tuple-element.10.knew_ref, f32[4,32,128]{2,1,0:T(8,128)S(1)} %get-tuple-element.11.vnew_ref, ...), custom_call_target="tpu_custom_call" | custom-call | tf_op jit(solution)/shard_map/attend/pallas_call | solution.py:438
  25.9 48.8 %mlp.1 = bf16[128,1024]{1,0:T(8,128)(2,1)S(1)} custom-call(bf16[32,512]{1,0:T(8,128)(2,1)S(1)} %get-tuple-element.12.o_ref, bf16[128,1024]{1,0:T(8,128)(2,1)} %hid_hbm.3, bf16[1024]{0:T(1024)(128)(2,1)} %gain_hbm.3, bf16[512,1024]{1,0:T(8,128)(2,1)} %bitcast.14, bf16[1376,1024]{1,0:T(8,128)(2,1)} %bitcast.12, bf16[1376,1024]{1,0:T(8,128)(2,1)} %bitcast.13, ...), custom_call_target="tpu_custom_call" | custom-call | tf_op jit(solution)/shard_map/mlp/pallas_call | solution.py:456
  74.6 0.7 copy.19
Async XLA Ops:
  0.6 15.6 %copy-start = (bf16[32,256,4,128]{3,2,1,0:T(4,128)(2,1)S(1)}, bf16[32,256,4,128]{3,2,1,0:T(4,128)(2,1)}, u32[]{:S(2)}) copy-start(bf16[32,256,4,128]{3,2,1,0:T(4,128)(2,1)} %param.25) | copy-start | bytes 25165828
  0.6 15.6 %copy-start.1 = (bf16[32,256,4,128]{3,2,1,0:T(4,128)(2,1)S(1)}, bf16[32,256,4,128]{3,2,1,0:T(4,128)(2,1)}, u32[]{:S(2)}) copy-start(bf16[32,256,4,128]{3,2,1,0:T(4,128)(2,1)} %param.26) | copy-start | bytes 25165828
  0.7 15.6 %copy-start.2 = (s32[32]{0:T(128)S(1)}, s32[32]{0:T(128)}, u32[]{:S(2)}) copy-start(s32[32]{0:T(128)} %len_ref.1) | copy-start | bytes 388
